TPU v7x, 16 devices: a 4x2x1 block of a 4x4x8 slice. The times are simulated.
16 devices in a mesh: dp: 2 (over y, z), tp: 8 (over x, core).
Axes of the slice: x: 4, y: 2, z: 1, core: 2. Of those that a mesh axis runs over, the one named last changes fastest.
The devices are a block of a 4x4x8 slice.
Arguments:
- tokens: int32 [96], P('dp'), parts along dimension 0
- positions: int32 [96], P('dp'), parts along dimension 0
- self_keys: bfloat16 [2, 96, 448, 8, 64], P(None, 'dp', None, 'tp'), parts along dimension 1
- self_vals: bfloat16 [2, 96, 448, 8, 64], P(None, 'dp', None, 'tp'), parts along dimension 1
- cross_keys: bfloat16 [2, 96, 1500, 8, 64], P(None, 'dp', None, 'tp'), parts along dimension 1
- cross_vals: bfloat16 [2, 96, 1500, 8, 64], P(None, 'dp', None, 'tp'), parts along dimension 1
- embed_table: bfloat16 [52224, 512], P('tp')
- pos_table: bfloat16 [448, 512], replicated
- w_qkv: bfloat16 [2, 512, 3, 8, 64], P(None, None, None, 'tp')
- w_cq: bfloat16 [2, 512, 8, 64], P(None, None, 'tp')
- in_bias: float32 [2, 3, 8, 64], P(None, None, 'tp')
- w_out: bfloat16 [2, 2, 8, 64, 512], P(None, None, 'tp')
- out_bias: float32 [2, 3, 512], replicated
- w_fc1: bfloat16 [2, 512, 2048], P(None, None, 'tp')
- b_fc1: float32 [2, 2048], P(None, 'tp')
- w_fc2: bfloat16 [2, 2048, 512], P(None, 'tp')
- ln_layers: float32 [2, 3, 2, 512], replicated
- ln_final: float32 [2, 512], replicated
Outputs:
- output 1: float32 [96, 52224], P('dp', 'tp'), parts along dimension 0
- output 2: bfloat16 [2, 96, 448, 8, 64], P(None, 'dp', None, 'tp'), parts along dimension 1
- output 3: bfloat16 [2, 96, 448, 8, 64], P(None, 'dp', None, 'tp'), parts along dimension 1
There are 2 independent parts. A program takes and returns all parts, laid end to end along the dimension named above; an argument that names none is the same for every part.
All inputs are finite; a program needn't handle non-finite values.
Results may differ from a plain program's by a relative error of at most 0.0123317.
Values are sent between devices in bfloat16 or wider.
A program may use at most 768 MiB of HBM per device.

v0:
```python
import jax
import jax.numpy as jnp
from jax import lax
from jax.sharding import PartitionSpec as P


def layer_norm(residual, ln_gain, ln_shift):
    row_mean = jnp.mean(residual, axis=-1, keepdims=True)
    centred = residual - row_mean
    variance = jnp.mean(centred * centred, axis=-1, keepdims=True)
    return (centred * lax.rsqrt(variance + 1e-5) * ln_gain + ln_shift).astype(jnp.bfloat16)


def cross_attend(queries, key_rows, val_rows):
    scores = jnp.einsum('bhe,bthe->bht', queries, key_rows, preferred_element_type=jnp.float32) * (queries.shape[-1] ** -0.5)
    weights = jax.nn.softmax(scores, axis=-1).astype(jnp.bfloat16)
    return jnp.einsum('bht,bthe->bhe', weights, val_rows, preferred_element_type=jnp.float32).astype(jnp.bfloat16)


def self_attend(queries, key_new, val_new, cache_keys, cache_vals, mask_add):
    qk_scale = queries.shape[-1] ** -0.5
    past_scores = jnp.einsum('bhe,bthe->bht', queries, cache_keys, preferred_element_type=jnp.float32) * qk_scale + mask_add
    new_score = jnp.einsum('bhe,bhe->bh', queries, key_new, preferred_element_type=jnp.float32)[:, :, None] * qk_scale
    score_peak = jnp.maximum(jnp.max(past_scores, axis=-1, keepdims=True), new_score)
    past_exp = jnp.exp(past_scores - score_peak)
    new_exp = jnp.exp(new_score - score_peak)
    denominator = jnp.sum(past_exp, axis=-1, keepdims=True) + new_exp
    past_weight = (past_exp / denominator).astype(jnp.bfloat16)
    new_weight = (new_exp / denominator).astype(jnp.bfloat16)
    mixed_vals = jnp.einsum('bht,bthe->bhe', past_weight, cache_vals, preferred_element_type=jnp.float32)
    mixed_vals = mixed_vals + new_weight.astype(jnp.float32) * val_new.astype(jnp.float32)
    return mixed_vals.astype(jnp.bfloat16)


def group_sum(part_sum):
    return lax.psum(part_sum, 'tp').astype(jnp.bfloat16).astype(jnp.float32)


def solution(mesh):
    def local_step(tokens, positions, self_keys, self_vals, cross_keys, cross_vals, embed_table, pos_table, w_qkv, w_cq, in_bias, w_out, out_bias, w_fc1, b_fc1, w_fc2, ln_layers, ln_final):
        shard_rows = embed_table.shape[0]
        local_ids = tokens - lax.axis_index('tp') * shard_rows
        owned_mask = (local_ids >= 0) & (local_ids < shard_rows)
        picked = jnp.take(embed_table, jnp.clip(local_ids, 0, shard_rows - 1), axis=0)
        picked = jnp.where(owned_mask[:, None], picked, jnp.zeros_like(picked))
        residual = lax.psum(picked, 'tp').astype(jnp.float32) + jnp.take(pos_table, positions, axis=0).astype(jnp.float32)
        cache_pos = jnp.arange(self_keys.shape[2])[None, :]
        mask_add = jnp.where(cache_pos < positions[:, None], 0.0, -1e30)[:, None, :]
        new_key_rows = []
        new_val_rows = []
        for layer_idx in range(self_keys.shape[0]):
            ln_params = ln_layers[layer_idx]
            bias_in = in_bias[layer_idx]
            hidden = layer_norm(residual, ln_params[0, 0], ln_params[0, 1])
            projected = jnp.einsum('bd,dthe->bthe', hidden, w_qkv[layer_idx], preferred_element_type=jnp.float32)
            queries = (projected[:, 0] + bias_in[0]).astype(jnp.bfloat16)
            key_new = projected[:, 1].astype(jnp.bfloat16)
            val_new = (projected[:, 2] + bias_in[1]).astype(jnp.bfloat16)
            attended = self_attend(queries, key_new, val_new, self_keys[layer_idx], self_vals[layer_idx], mask_add)
            head_sum = jnp.einsum('bhe,hed->bd', attended, w_out[layer_idx, 0], preferred_element_type=jnp.float32)
            residual = residual + group_sum(head_sum) + out_bias[layer_idx, 0]
            hidden = layer_norm(residual, ln_params[1, 0], ln_params[1, 1])
            cross_q = (jnp.einsum('bd,dhe->bhe', hidden, w_cq[layer_idx], preferred_element_type=jnp.float32) + bias_in[2]).astype(jnp.bfloat16)
            attended = cross_attend(cross_q, cross_keys[layer_idx], cross_vals[layer_idx])
            head_sum = jnp.einsum('bhe,hed->bd', attended, w_out[layer_idx, 1], preferred_element_type=jnp.float32)
            residual = residual + group_sum(head_sum) + out_bias[layer_idx, 1]
            hidden = layer_norm(residual, ln_params[2, 0], ln_params[2, 1])
            fc1_out = jnp.dot(hidden, w_fc1[layer_idx], preferred_element_type=jnp.float32) + b_fc1[layer_idx]
            active = jax.nn.gelu(fc1_out, approximate=False).astype(jnp.bfloat16)
            fc2_out = jnp.dot(active, w_fc2[layer_idx], preferred_element_type=jnp.float32)
            residual = residual + group_sum(fc2_out) + out_bias[layer_idx, 2]
            new_key_rows.append(key_new)
            new_val_rows.append(val_new)
        final_hidden = layer_norm(residual, ln_final[0], ln_final[1])
        logits = jnp.einsum('bd,vd->bv', final_hidden, embed_table, preferred_element_type=jnp.float32)
        write_mask = (cache_pos == positions[:, None])[None, :, :, None, None]
        new_keys = jnp.where(write_mask, jnp.stack(new_key_rows)[:, :, None], self_keys)
        new_vals = jnp.where(write_mask, jnp.stack(new_val_rows)[:, :, None], self_vals)
        return logits, new_keys, new_vals

    batch_spec = P('dp')
    cache_spec = P(None, 'dp', None, 'tp', None)
    in_specs = (batch_spec, batch_spec, cache_spec, cache_spec, cache_spec, cache_spec, P('tp', None), P(None, None), P(None, None, None, 'tp', None), P(None, None, 'tp', None), P(None, None, 'tp', None), P(None, None, 'tp', None, None), P(None, None, None), P(None, None, 'tp'), P(None, 'tp'), P(None, 'tp', None), P(None, None, None, None), P(None, None))
    out_specs = (P('dp', 'tp'), cache_spec, cache_spec)
    return jax.shard_map(local_step, mesh=mesh, in_specs=in_specs, out_specs=out_specs, check_vma=False)
```

profile of v0, /device:TPU:113, one launch (start us, length us, event | category | flops | bytes accessed | tf_op | source)
XLA Modules:
  0.0 241.7 jit_solution(2441606271163096001)
XLA Ops:
  4.3 0.8 fusion.292
  5.0 0.8 fusion.291
  8.0 4.4 %gather_fusion = bf16[48,512]{1,0:T(8,128)(2,1)S(1)} fusion(bf16[6528,512]{1,0:T(8,128)(2,1)} %param.24, s32[1024]{0:T(1024)S(1)} %pad_clamp_fusion.1), kind=kCustom, calls=%fused_computation | custom fusion | bytes 98496 | tf_op jit(solution)/shard_map/jit(_take)/gather | solution.py:44
  12.5 24.5 %psum.49 = bf16[48,512]{1,0:T(8,128)(2,1)S(1)} all-reduce(bf16[48,512]{1,0:T(8,128)(2,1)S(1)} %select_select_fusion), channel_id=1, replica_groups=mesh['dp'=2,'tp'=8] {'tp'}, use_global_device_ids=true, to_apply=%region_0.1 | all-reduce | flops 24576 | bytes 98304 | tf_op jit(solution)/shard_map/psum | solution.py:46
  37.4 1.2 fusion.44
  38.7 2.4 fusion.18
  41.1 0.9 fusion.281
  42.0 0.9 fusion.49
  42.9 0.8 fusion.119
  43.6 2.8 %fusion.16 = f32[48,1,64]{2,1,0:T(1,128)S(1)} fusion(bf16[2,48,448,1,64]{2,4,3,1,0:T(8,128)(2,1)} %param.21, bf16[48,448,1]{1,0,2:T(8,128)(2,1)S(1)} %fusion.119), kind=kOutput, calls=%fused_computation.20 | convolution fusion | flops 2752512 | bytes 3201024 | tf_op jit(solution)/shard_map/bht,bthe->bhe/dot_general | solution.py:30
  46.6 24.7 %psum.50 = bf16[48,512]{1,0:T(8,128)(2,1)S(1)} all-reduce(f32[48,512]{1,0:T(8,128)S(1)} %fusion.60), channel_id=1, replica_groups=mesh['dp'=2,'tp'=8] {'tp'}, use_global_device_ids=true, to_apply=%region_5.6 | all-reduce | flops 24576 | bytes 147456 | tf_op jit(solution)/shard_map/psum | solution.py:36
  72.0 5.0 %fusion.6 = f32[48,1,1500]{2,1,0:T(1,128)S(1)} fusion(bf16[2,48,1500,1,64]{2,4,3,1,0:T(8,128)(2,1)} %param.22, bf16[48,64,1]{1,0,2:T(8,128)(2,1)S(1)} %fusion.27), kind=kOutput, calls=%fused_computation.8 | convolution fusion | flops 9216000 | bytes 9731328 | tf_op jit(solution)/shard_map/bhe,bthe->bht/dot_general | solution.py:15
  77.5 6.2 %fusion.4 = f32[48,1,64]{2,1,0:T(1,128)S(1)} fusion(bf16[2,48,1500,1,64]{2,4,3,1,0:T(8,128)(2,1)} %param.23, bf16[48,1500,1]{1,0,2:T(8,128)(2,1)S(1)} %fusion.45), kind=kOutput, calls=%fused_computation.6 | convolution fusion | flops 9216000 | bytes 9593472 | tf_op jit(solution)/shard_map/bht,bthe->bhe/dot_general | solution.py:17
  83.9 24.4 %psum.51 = bf16[48,512]{1,0:T(8,128)(2,1)S(1)} all-reduce(f32[48,512]{1,0:T(8,128)S(1)} %fusion.57), channel_id=1, replica_groups=mesh['dp'=2,'tp'=8] {'tp'}, use_global_device_ids=true, to_apply=%region_10.11 | all-reduce | flops 24576 | bytes 147456 | tf_op jit(solution)/shard_map/psum | solution.py:36
  109.2 24.4 %psum.52 = bf16[48,512]{1,0:T(8,128)(2,1)S(1)} all-reduce(f32[48,512]{1,0:T(8,128)S(1)} %fusion.33), channel_id=1, replica_groups=mesh['dp'=2,'tp'=8] {'tp'}, use_global_device_ids=true, to_apply=%region_13.14 | all-reduce | flops 24576 | bytes 147456 | tf_op jit(solution)/shard_map/psum | solution.py:36
  134.3 2.4 fusion.14
  137.3 2.8 %fusion.12 = f32[48,1,64]{2,1,0:T(1,128)S(1)} fusion(bf16[2,48,448,1,64]{2,4,3,1,0:T(8,128)(2,1)} %param.21, bf16[48,448,1]{1,0,2:T(8,128)(2,1)S(1)} %fusion.120), kind=kOutput, calls=%fused_computation.16 | convolution fusion | flops 2752512 | bytes 3201024 | tf_op jit(solution)/shard_map/bht,bthe->bhe/dot_general | solution.py:30
  140.3 24.4 %psum.53 = bf16[48,512]{1,0:T(8,128)(2,1)S(1)} all-reduce(f32[48,512]{1,0:T(8,128)S(1)} %fusion.55), channel_id=1, replica_groups=mesh['dp'=2,'tp'=8] {'tp'}, use_global_device_ids=true, to_apply=%region_18.19 | all-reduce | flops 24576 | bytes 147456 | tf_op jit(solution)/shard_map/psum | solution.py:36
  165.2 5.0 %fusion.2 = f32[48,1,1500]{2,1,0:T(1,128)S(1)} fusion(bf16[2,48,1500,1,64]{2,4,3,1,0:T(8,128)(2,1)} %param.22, bf16[48,64,1]{1,0,2:T(8,128)(2,1)S(1)} %fusion.26), kind=kOutput, calls=%fused_computation.4 | convolution fusion | flops 9216000 | bytes 9731328 | tf_op jit(solution)/shard_map/bhe,bthe->bht/dot_general | solution.py:15
  170.8 6.2 %fusion = f32[48,1,64]{2,1,0:T(1,128)S(1)} fusion(bf16[2,48,1500,1,64]{2,4,3,1,0:T(8,128)(2,1)} %param.23, bf16[48,1500,1]{1,0,2:T(8,128)(2,1)S(1)} %fusion.46), kind=kOutput, calls=%fused_computation.2 | convolution fusion | flops 9216000 | bytes 9593472 | tf_op jit(solution)/shard_map/bht,bthe->bhe/dot_general | solution.py:17
  177.1 24.6 %psum.54 = bf16[48,512]{1,0:T(8,128)(2,1)S(1)} all-reduce(f32[48,512]{1,0:T(8,128)S(1)} %fusion.52), channel_id=1, replica_groups=mesh['dp'=2,'tp'=8] {'tp'}, use_global_device_ids=true, to_apply=%region_23.24 | all-reduce | flops 24576 | bytes 147456 | tf_op jit(solution)/shard_map/psum | solution.py:36
  202.5 24.6 %psum.55 = bf16[48,512]{1,0:T(8,128)(2,1)S(1)} all-reduce(f32[48,512]{1,0:T(8,128)S(1)} %fusion.30), channel_id=1, replica_groups=mesh['dp'=2,'tp'=8] {'tp'}, use_global_device_ids=true, to_apply=%region_26.27 | all-reduce | flops 24576 | bytes 147456 | tf_op jit(solution)/shard_map/psum | solution.py:36
  227.4 6.2 %fusion.78 = f32[48,6528]{1,0:T(8,128)} fusion(bf16[6528,512]{1,0:T(8,128)(2,1)} %param.24, f32[48,512]{1,0:T(8,128)S(1)} %get-tuple-element.4, f32[512]{0:T(512)S(1)} %bitcast.246, f32[512]{0:T(512)S(1)} %bitcast.245, f32[48]{0:T(128)S(1)} %add_rsqrt_fusion, f32[48]{0:T(128)S(1)} %broadcast_multiply_fusion), kind=kOutput, calls=%fused_computation.126 | convolution fusion | flops 320987136 | bytes 8040832 | tf_op jit(solution)/shard_map/bd,vd->bv/dot_general | solution.py:75
  233.6 8.1 %broadcast_select_fusion = (bf16[2,48,448,1,64]{2,4,3,1,0:T(8,128)(2,1)}, bf16[2,48,448,1,64]{2,4,3,1,0:T(8,128)(2,1)}) fusion(bf16[2,48,448,1,64]{2,4,3,1,0:T(8,128)(2,1)} %param.21, pred[48,448]{1,0:T(8,128)(4,1)S(1)} %iota_compare_fusion, bf16[2,48,64]{2,1,0:T(8,128)(2,1)S(1)} %maximum_bitcast_fusion.1, bf16[2,48,448,1,64]{2,4,3,1,0:T(8,128)(2,1)S(1)} %bitcast.239, ...), kind=kLoop, calls=%fused_computation.14 | loop fusion | flops 5505024 | bytes 22066176 | tf_op jit(solution)/shard_map/jit(_where)/select_n | solution.py:78
  (91 shorter events, 12.3 us)
Async XLA Ops:
  0.6 6.7 %copy-start = (bf16[448,512]{1,0:T(8,128)(2,1)S(1)}, bf16[448,512]{1,0:T(8,128)(2,1)}, u32[]{:S(2)}) copy-start(bf16[448,512]{1,0:T(8,128)(2,1)} %param.25) | copy-start | bytes 1376260
  0.6 45.8 %copy-start.2 = (bf16[2,2,1,64,512]{4,3,2,1,0:T(8,128)(2,1)S(1)}, bf16[2,2,1,64,512]{4,3,2,1,0:T(8,128)(2,1)}, u32[]{:S(2)}) copy-start(bf16[2,2,1,64,512]{4,3,2,1,0:T(8,128)(2,1)} %param.29) | copy-start | bytes 786436
  0.7 71.1 %copy-start.7 = (bf16[2,512,1,64]{1,3,2,0:T(8,128)(2,1)S(1)}, bf16[2,512,1,64]{1,3,2,0:T(8,128)(2,1)}, u32[]{:S(2)}) copy-start(bf16[2,512,1,64]{1,3,2,0:T(8,128)(2,1)} %param.27) | copy-start | bytes 393220
  77.1 31.5 %copy-start.4 = (bf16[2,256,512]{2,1,0:T(8,128)(2,1)S(1)}, bf16[2,256,512]{2,1,0:T(8,128)(2,1)}, u32[]{:S(2)}) copy-start(bf16[2,256,512]{2,1,0:T(8,128)(2,1)} %param.33) | copy-start | bytes 1572868
  77.1 31.5 %copy-start.5 = (bf16[2,512,256]{2,1,0:T(8,128)(2,1)S(1)}, bf16[2,512,256]{2,1,0:T(8,128)(2,1)}, u32[]{:S(2)}) copy-start(bf16[2,512,256]{2,1,0:T(8,128)(2,1)} %param.31) | copy-start | bytes 1572868
  77.5 56.4 %copy-start.6 = (bf16[2,512,3,1,64]{1,4,3,2,0:T(8,128)(2,1)S(1)}, bf16[2,512,3,1,64]{1,4,3,2,0:T(8,128)(2,1)}, u32[]{:S(2)}) copy-start(bf16[2,512,3,1,64]{1,4,3,2,0:T(8,128)(2,1)} %param.26) | copy-start | bytes 1179652
  77.5 59.2 %copy-start.3 = (s32[48]{0:T(128)S(1)}, s32[48]{0:T(128)}, u32[]{:S(2)}) copy-start(s32[48]{0:T(128)} %param.19) | copy-start | bytes 580
  202.5 31.1 %slice-start = ((s8[6291456]{0:T(1024)(128)(4,1)}), s8[2097152]{0:T(1024)(128)(4,1)S(1)}, s32[]{:S(2)}) async-start(s8[6291456]{0:T(1024)(128)(4,1)} %bitcast.238), calls=%async_computation | async-start | bytes 4194304
  227.4 6.2 %slice-start.1 = ((s8[6291456]{0:T(1024)(128)(4,1)}), s8[4194304]{0:T(1024)(128)(4,1)S(1)}, s32[]{:S(2)}) async-start(s8[6291456]{0:T(1024)(128)(4,1)} %bitcast.238), calls=%async_computation.1 | async-start | bytes 8388608
  233.6 8.1 %copy-start.1 = (bf16[448,512]{1,0:T(8,128)(2,1)S(1)}, bf16[448,512]{1,0:T(8,128)(2,1)}, u32[]{:S(2)}) copy-start(bf16[448,512]{1,0:T(8,128)(2,1)} %param.25) | copy-start | bytes 1376260
where the time goes:
time: 245 us; the launch traced here: 242 us
  blocking collectives  172 us (70%)
  matrix products  42.6 us (17%)
  other arithmetic  17.6 us (7%)
  local copies, waits for them, and re-layouts  8.97 us (4%)
    psum x6, blocking collectives, group_sum(): return lax.psum(part_sum, 'tp').astype(jnp.bfloat16).astype(jnp.float32)  147 us
    psum x1, blocking collectives, local_step(): lax.psum(picked, 'tp').astype(jnp.float32)  24.5 us
    dot_general x2, matrix products, cross_attend(): jnp.einsum('bht,bthe->bhe', weights, val_rows, preferred_element_type=jnp...  12.5 us
    dot_general x2, matrix products, cross_attend(): jnp.einsum('bhe,bthe->bht', queries, key_rows, preferred_element_type=jnp...  10 us
    select_n x1, other arithmetic, local_step(): jnp.where(write_mask, jnp.stack(new_val_rows)[:, :, None], self_vals)  8.08 us
    dot_general x1, matrix products, local_step(): jnp.einsum('bd,vd->bv', final_hidden, embed_table, preferred_element_type...  6.19 us
    dot_general x2, matrix products, self_attend(): jnp.einsum('bht,bthe->bhe', past_weight, cache_vals, preferred_element_ty...  5.59 us

commit v1 on v0

v1 whole, which is shorter than its diff:
```python
import functools

import jax
import jax.numpy as jnp
from jax import lax
from jax.experimental import pallas as pl
from jax.experimental.pallas import tpu as pltpu
from jax.sharding import PartitionSpec as P

MESH = pl.DeviceIdType.MESH
GROUP = 16
F32 = jnp.float32
BF16 = jnp.bfloat16
NT = (((1,), (1,)), ((), ()))


def dot_nt(a, b):
    return lax.dot_general(a, b, NT, preferred_element_type=F32)


def dot_nn(a, b):
    return jnp.dot(a, b, preferred_element_type=F32)


def layer_norm(x, gain, shift):
    mean = jnp.mean(x, axis=-1, keepdims=True)
    centred = x - mean
    variance = jnp.mean(centred * centred, axis=-1, keepdims=True)
    return (centred * lax.rsqrt(variance + 1e-5) * gain + shift).astype(BF16)


def step_kernel(
    n, emb, pos_rows, positions, w_qkv, w_cq, in_bias, out_bias, fc1, b_fc1, ln_layers, ln_final, w_out, fc2,
    self_k, self_v, cross_k, cross_v,
    final_out, knew_out, vnew_out,
    sk, sv, ck, cv, wo_full, fc2_full, emb_slots, o_slots, act_slots, q_bd, scores,
    sem_sk, sem_sv, sem_ck, sem_cv, sem_w, emb_send, emb_recv, o_send, o_recv, act_send, act_recv, w_send, w_recv,
):
    layers, batch = sk.shape[0], emb.shape[0]
    head = w_cq.shape[1]
    span = GROUP * head
    me = lax.axis_index("tp")
    partner = me + 1 - 2 * lax.rem(me, 2)

    def peer(k):
        return lax.rem(me + k, n)

    barrier = pltpu.get_barrier_semaphore()
    for k in range(1, n):
        pl.semaphore_signal(barrier, 1, device_id={"tp": peer(k)}, device_id_type=MESH)
    pl.semaphore_wait(barrier, n - 1)

    def remote(src, dst, send, recv, to):
        return pltpu.make_async_remote_copy(src, dst, send, recv, device_id={"tp": to}, device_id_type=MESH)

    order = sorted(range(1, n), key=lambda k: -min(k, n - k))

    def send_all(src, slots, send, recv):
        copies = [remote(src, slots.at[me], send.at[k], recv.at[me], peer(k)) for k in order]
        for c in copies:
            c.start()
        return copies

    def wait_all(copies, src, slots, send, recv):
        for k in order:
            j = peer(k)
            remote(src, slots.at[j], send.at[k], recv.at[j], j).wait_recv()
        for c in copies:
            c.wait_send()

    wo_parts = [(w_out.at[l, a], wo_full.at[l, a]) for l in range(layers) for a in range(2)]
    fc2_parts = [(fc2.at[l], fc2_full.at[l]) for l in range(layers)]
    parts = [wo_parts[0], wo_parts[1], fc2_parts[0], wo_parts[2], wo_parts[3], fc2_parts[1]]
    own_copies, first_hop, second_hop = {}, {}, {}

    def weights_start(i):
        src, full = parts[i]
        own_copies[i] = pltpu.make_async_copy(src, full.at[me], sem_w.at[i])
        own_copies[i].start()
        first_hop[i] = [remote(src, full.at[me], w_send.at[i, k], w_recv.at[i, me], peer(k)) for k in range(2, n, 2)]
        first_hop[i].append(remote(src, full.at[me], w_send.at[i, 1], w_recv.at[i, me], partner))
        for c in first_hop[i]:
            c.start()

    def weights_forward(i):
        src, full = parts[i]
        second_hop[i] = []
        for k in range(2, n, 2):
            j = peer(k)
            remote(src, full.at[j], w_send.at[i, k], w_recv.at[i, j], j).wait_recv()
            c = remote(full.at[j], full.at[j], w_send.at[i, k + 1], w_recv.at[i, j], partner)
            c.start()
            second_hop[i].append(c)

    def weights_wait(i):
        src, full = parts[i]
        remote(src, full.at[partner], w_send.at[i, 1], w_recv.at[i, partner], partner).wait_recv()
        for k in range(2, n, 2):
            j = lax.rem(partner + k, n)
            remote(src, full.at[j], w_send.at[i, k + 1], w_recv.at[i, j], partner).wait_recv()
        for c in first_hop[i] + second_hop[i]:
            c.wait_send()
        own_copies[i].wait()

    emb_copies = send_all(emb, emb_slots, emb_send, emb_recv)
    weights_start(0)

    loads = {}
    for l in range(layers):
        for name, src, dst, sem in (("sk", self_k, sk, sem_sk), ("sv", self_v, sv, sem_sv), ("ck", cross_k, ck, sem_ck), ("cv", cross_v, cv, sem_cv)):
            loads[name, l] = pltpu.make_async_copy(src.at[l], dst.at[l], sem.at[l])
            loads[name, l].start()
    weights_start(1)

    emb_slots[me] = emb[...]
    wait_all(emb_copies, emb, emb_slots, emb_send, emb_recv)
    x = emb_slots[0].astype(F32)
    for j in range(1, n):
        x = x + emb_slots[j].astype(F32)
    x = x + pos_rows[...].astype(F32)

    row = lax.broadcasted_iota(jnp.int32, (batch, span), 0)
    col = lax.broadcasted_iota(jnp.int32, (batch, span), 1)
    diagonal = lax.rem(row, GROUP) == lax.div(col, head)
    group_diagonal = diagonal[:GROUP]

    def attend(q, keys, vals, finish):
        length = keys.shape[2]
        wide = jnp.concatenate([q] * GROUP, axis=1)
        q_bd[...] = jnp.where(diagonal, wide, 0).astype(BF16)
        for g in range(batch // GROUP):
            rows = slice(g * GROUP, (g + 1) * GROUP)
            scores[rows, :length] = dot_nn(q_bd[rows], keys[rows].reshape(span, length))
        weights, extra = finish(scores[:, :length] * (head ** -0.5))
        out = []
        for g in range(batch // GROUP):
            rows = slice(g * GROUP, (g + 1) * GROUP)
            full = dot_nt(weights[rows], vals[rows].reshape(span, length))
            full = jnp.where(group_diagonal, full, 0.0)
            while full.shape[1] > head:
                half = full.shape[1] // 2
                full = full[:, :half] + full[:, half:]
            out.append(full)
        return jnp.concatenate(out, axis=0) + extra

    def exchange_heads(e, attended):
        slots, send, recv = o_slots.at[e], o_send.at[e], o_recv.at[e]
        slots[me] = attended
        return send_all(slots.at[me], slots, send, recv)

    def gathered_heads(e, copies):
        slots, send, recv = o_slots.at[e], o_send.at[e], o_recv.at[e]
        wait_all(copies, slots.at[me], slots, send, recv)
        return jnp.concatenate([slots[j] for j in range(n)], axis=1)

    def project(heads, w, bias):
        return dot_nn(heads, w[...].reshape(n * head, -1)).astype(BF16).astype(F32), bias

    for l in range(layers):
        ln = ln_layers[l]
        h = layer_norm(x, ln[0, 0:1], ln[0, 1:2])
        q = (dot_nt(h, w_qkv[l, 0]) + in_bias[l, 0:1]).astype(BF16)
        k_new = dot_nt(h, w_qkv[l, 1]).astype(BF16)
        v_new = (dot_nt(h, w_qkv[l, 2]) + in_bias[l, 1:2]).astype(BF16)
        knew_out[l] = k_new
        vnew_out[l] = v_new
        loads["sk", l].wait()
        loads["sv", l].wait()
        new_score = jnp.sum(q.astype(F32) * k_new.astype(F32), axis=-1, keepdims=True) * (head ** -0.5)

        def finish_self(s):
            place = lax.broadcasted_iota(jnp.int32, s.shape, 1)
            s = jnp.where(place < positions[...], s, -1e30)
            peak = jnp.maximum(jnp.max(s, axis=-1, keepdims=True), new_score)
            e = jnp.exp(s - peak)
            e_new = jnp.exp(new_score - peak)
            total = jnp.sum(e, axis=-1, keepdims=True) + e_new
            return (e / total).astype(BF16), (e_new / total).astype(BF16).astype(F32) * v_new.astype(F32)

        def finish_cross(s):
            e = jnp.exp(s - jnp.max(s, axis=-1, keepdims=True))
            return (e / jnp.sum(e, axis=-1, keepdims=True)).astype(BF16), 0.0

        attended = attend(q, sk.at[l], sv.at[l], finish_self).astype(BF16)
        copies = exchange_heads(2 * l, attended)
        weights_start(3 * l + 2)
        weights_forward(3 * l)
        weights_wait(3 * l)
        heads = gathered_heads(2 * l, copies)
        x = x + dot_nn(heads, wo_full[l, 0].reshape(n * head, -1)).astype(BF16).astype(F32) + out_bias[l, 0:1]

        h = layer_norm(x, ln[1, 0:1], ln[1, 1:2])
        q = (dot_nt(h, w_cq[l]) + in_bias[l, 2:3]).astype(BF16)
        loads["ck", l].wait()
        loads["cv", l].wait()
        attended = attend(q, ck.at[l], cv.at[l], finish_cross).astype(BF16)
        copies = exchange_heads(2 * l + 1, attended)
        weights_forward(3 * l + 1)
        weights_wait(3 * l + 1)
        heads = gathered_heads(2 * l + 1, copies)
        x = x + dot_nn(heads, wo_full[l, 1].reshape(n * head, -1)).astype(BF16).astype(F32) + out_bias[l, 1:2]

        h = layer_norm(x, ln[2, 0:1], ln[2, 1:2])
        hidden = dot_nn(h, fc1[l]) + b_fc1[l : l + 1]
        active = (0.5 * hidden * (1.0 + lax.erf(hidden * (0.5 ** 0.5)))).astype(BF16)
        slots, send, recv = act_slots.at[l], act_send.at[l], act_recv.at[l]
        slots[me] = active
        copies = send_all(slots.at[me], slots, send, recv)
        weights_forward(3 * l + 2)
        weights_wait(3 * l + 2)
        if l + 1 < layers:
            weights_start(3 * l + 3)
            weights_start(3 * l + 4)
        wait_all(copies, slots.at[me], slots, send, recv)
        total = dot_nn(slots[0], fc2_full[l, 0])
        for j in range(1, n):
            total = total + dot_nn(slots[j], fc2_full[l, j])
        x = x + total.astype(BF16).astype(F32) + out_bias[l, 2:3]

    final_out[...] = layer_norm(x, ln_final[0:1], ln_final[1:2])


def solution(mesh):
    n = mesh.shape["tp"]

    def local_step(tokens, positions, self_keys, self_vals, cross_keys, cross_vals, embed_table, pos_table, w_qkv, w_cq, in_bias, w_out, out_bias, w_fc1, b_fc1, w_fc2, ln_layers, ln_final):
        layers, batch, ctx, _, head = self_keys.shape
        frames = cross_keys.shape[2]
        width = embed_table.shape[1]
        hidden = w_fc1.shape[2]
        shard_rows = embed_table.shape[0]
        local_ids = tokens - lax.axis_index("tp") * shard_rows
        owned = (local_ids >= 0) & (local_ids < shard_rows)
        picked = jnp.take(embed_table, jnp.clip(local_ids, 0, shard_rows - 1), axis=0)
        picked = jnp.where(owned[:, None], picked, jnp.zeros_like(picked))
        pos_rows = jnp.take(pos_table, positions, axis=0)

        def by_place(cache):
            return jnp.transpose(cache[:, :, :, 0, :], (0, 1, 3, 2))

        vmem = pl.BlockSpec(memory_space=pltpu.VMEM)
        hbm = pl.BlockSpec(memory_space=pl.ANY)
        rows = jax.ShapeDtypeStruct((layers, batch, head), BF16)
        final_hidden, k_new, v_new = pl.pallas_call(
            functools.partial(step_kernel, n),
            out_shape=(jax.ShapeDtypeStruct((batch, width), BF16), rows, rows),
            in_specs=[vmem] * 11 + [hbm] * 6,
            out_specs=(vmem, vmem, vmem),
            scratch_shapes=[
                pltpu.VMEM((layers, batch, head, ctx), BF16),
                pltpu.VMEM((layers, batch, head, ctx), BF16),
                pltpu.VMEM((layers, batch, head, frames), BF16),
                pltpu.VMEM((layers, batch, head, frames), BF16),
                pltpu.VMEM((layers, 2, n, head, width), BF16),
                pltpu.VMEM((layers, n, hidden, width), BF16),
                pltpu.VMEM((n, batch, width), BF16),
                pltpu.VMEM((2 * layers, n, batch, head), BF16),
                pltpu.VMEM((layers, n, batch, hidden), BF16),
                pltpu.VMEM((batch, GROUP * head), BF16),
                pltpu.VMEM((batch, frames), F32),
                pltpu.SemaphoreType.DMA((layers,)),
                pltpu.SemaphoreType.DMA((layers,)),
                pltpu.SemaphoreType.DMA((layers,)),
                pltpu.SemaphoreType.DMA((layers,)),
                pltpu.SemaphoreType.DMA((3 * layers,)),
                pltpu.SemaphoreType.DMA((n,)),
                pltpu.SemaphoreType.DMA((n,)),
                pltpu.SemaphoreType.DMA((2 * layers, n)),
                pltpu.SemaphoreType.DMA((2 * layers, n)),
                pltpu.SemaphoreType.DMA((layers, n)),
                pltpu.SemaphoreType.DMA((layers, n)),
                pltpu.SemaphoreType.DMA((3 * layers, n)),
                pltpu.SemaphoreType.DMA((3 * layers, n)),
            ],
            compiler_params=pltpu.CompilerParams(collective_id=0, has_side_effects=True, vmem_limit_bytes=63 * 1024 * 1024),
            name="decode_step",
        )(
            picked, pos_rows, positions[:, None],
            jnp.transpose(w_qkv[:, :, :, 0, :], (0, 2, 3, 1)), jnp.transpose(w_cq[:, :, 0, :], (0, 2, 1)), in_bias[:, :, 0, :],
            out_bias, w_fc1, b_fc1, ln_layers, ln_final, w_out[:, :, 0], w_fc2,
            by_place(self_keys), by_place(self_vals), by_place(cross_keys), by_place(cross_vals),
        )
        logits = jnp.einsum("bd,vd->bv", final_hidden, embed_table, preferred_element_type=F32)
        write_mask = (jnp.arange(ctx)[None, :] == positions[:, None])[None, :, :, None, None]
        new_keys = jnp.where(write_mask, k_new[:, :, None, None, :], self_keys)
        new_vals = jnp.where(write_mask, v_new[:, :, None, None, :], self_vals)
        return logits, new_keys, new_vals

    batch_spec = P("dp")
    cache_spec = P(None, "dp", None, "tp", None)
    in_specs = (batch_spec, batch_spec, cache_spec, cache_spec, cache_spec, cache_spec, P("tp", None), P(None, None), P(None, None, None, "tp", None), P(None, None, "tp", None), P(None, None, "tp", None), P(None, None, "tp", None, None), P(None, None, None), P(None, None, "tp"), P(None, "tp"), P(None, "tp", None), P(None, None, None, None), P(None, None))
    out_specs = (P("dp", "tp"), cache_spec, cache_spec)
    return jax.shard_map(local_step, mesh=mesh, in_specs=in_specs, out_specs=out_specs, check_vma=False)
```

time: 245 us -> 92 us (0.38); the launches traced: 242 us -> 91.7 us
  blocking collectives: 172 us -> 0 us
  Pallas kernels: 0 us -> 64.2 us
  matrix products: 42.6 us -> 3.13 us
  other arithmetic: 17.6 us -> 14.6 us
    psum x7 -> x0, blocking collectives: 172 us -> none  [the longest x6 147 us: group_sum(): return lax.psum(part_sum, 'tp').astype(jnp.bfloat16).astype(jnp.float32)]
    pallas_call x0 -> x1, Pallas kernels: none -> 64.2 us  [local_step(): pl.pallas_call(functools.partial(step_kernel, n), out_shape=(jax.ShapeDty...]
    dot_general x18 -> x0, matrix products: 36.4 us -> none  [the longest x2 12.5 us: cross_attend(): jnp.einsum('bht,bthe->bhe', weights, val_rows, preferred_element_type=jnp...]
    select_n x3, other arithmetic: 8.82 us -> 13.1 us  [the longest x1 11.7 us: local_step(): new_vals = jnp.where(write_mask, v_new[:, :, None, None, :], self_vals)]
    reduce_sum x18 -> x0, other arithmetic: 3.76 us -> none  [the longest x7 1.29 us: layer_norm(): variance = jnp.mean(centred * centred, axis=-1, keepdims=True)]
    dot_general x1, matrix products: 6.19 us -> 3.13 us  [local_step(): jnp.einsum('bd,vd->bv', final_hidden, embed_table, preferred_element_type...]
where the time goes in v1:
time: 92 us; the launch traced here: 91.7 us
  Pallas kernels  64.2 us (70%)
  other arithmetic  14.6 us (16%)
  local copies, waits for them, and re-layouts  9.07 us (10%)
  matrix products  3.13 us (3%)
    pallas_call x1, Pallas kernels, local_step(): pl.pallas_call(functools.partial(step_kernel, n), out_shape=(jax.ShapeDty...  64.2 us
    select_n x1, other arithmetic, local_step(): new_vals = jnp.where(write_mask, v_new[:, :, None, None, :], self_vals)  11.7 us
    gather x1, local copies, waits for them, and re-layouts, local_step(): jnp.take(embed_table, jnp.clip(local_ids, 0, shard_rows - 1), axis=0)  4.43 us
    dot_general x1, matrix products, local_step(): jnp.einsum('bd,vd->bv', final_hidden, embed_table, preferred_element_type...  3.13 us
    unnamed x12, local copies, waits for them, and re-layouts  2.03 us

profile of v1, /device:TPU:113, one launch (start us, length us, event | category | flops | bytes accessed | tf_op | source)
XLA Modules:
  0.0 91.7 jit_solution(8519049406784767528)
XLA Ops:
  0.6 0.0 copy-start
  0.7 0.7 compare_and_fusion.1
  1.4 4.4 %gather_fusion = bf16[48,512]{1,0:T(8,128)(2,1)S(1)} fusion(bf16[6528,512]{1,0:T(8,128)(2,1)} %param.24, s32[1024]{0:T(1024)S(1)} %pad_clamp_fusion.1), kind=kCustom, calls=%fused_computation | custom fusion | bytes 98496 | tf_op jit(solution)/shard_map/jit(_take)/gather | solution.py:234
  5.8 0.7 compare_select_fusion
  6.5 0.0 copy-done
  6.5 0.7 gather_fusion.1
  7.1 0.7 compare_and_fusion
  7.8 0.7 select_select_fusion
  8.5 1.3 %copy.24.positions = s32[48,1]{1,0:T(8,128)} copy(s32[48,1]{0,1:T(1,128)} %bitcast.33) | data formatting | bytes 384 | tf_op jit(solution)/shard_map/broadcast_in_dim | solution.py:278
  9.9 1.3 %copy.26.out_bias = f32[2,3,512]{2,1,0:T(4,128)} copy(f32[2,3,512]{2,0,1:T(2,128)} %param.30) | data formatting | bytes 24576 | tf_op args[12]
  11.2 0.7 copy.28
  11.9 0.6 copy.25.in_bias
  12.5 0.0 copy-start.4
  12.5 64.2 %decode_step.1 = (bf16[48,512]{1,0:T(8,128)(2,1)}, bf16[2,48,64]{2,1,0:T(8,128)(2,1)}, bf16[2,48,64]{2,1,0:T(8,128)(2,1)}) custom-call(bf16[48,512]{1,0:T(8,128)(2,1)} %get-tuple-element.14.emb, bf16[48,512]{1,0:T(8,128)(2,1)} %get-tuple-element.15.pos_rows, s32[48,1]{1,0:T(8,128)} %copy.24.positions, bf16[2,3,64,512]{3,2,1,0:T(8,128)(2,1)} %bitcast.29, ...), custom_call_target="tpu_custom_call" | custom-call | tf_op jit(solution)/shard_map/decode_step/pallas_call | solution.py:244
  76.7 0.0 copy-done.4
  76.8 0.1 iota_compare_fusion
  76.8 0.0 copy-start.2
  76.9 0.0 copy-start.3
  76.9 0.0 copy-start.1
  76.9 11.7 %broadcast_select_fusion = (bf16[2,48,448,1,64]{2,4,3,1,0:T(8,128)(2,1)}, bf16[2,48,448,1,64]{2,4,3,1,0:T(8,128)(2,1)}) fusion(bf16[2,48,448,1,64]{2,4,3,1,0:T(8,128)(2,1)} %param.21, pred[48,448]{1,0:T(8,128)(4,1)S(1)} %iota_compare_fusion, bf16[2,48,64]{2,1,0:T(8,128)(2,1)} %get-tuple-element.8, bf16[2,48,448,1,64]{2,4,3,1,0:T(8,128)(2,1)} %param.20, ...), kind=kLoop, calls=%fused_computation.2 | loop fusion | flops 5505024 | bytes 22066176 | tf_op jit(solution)/shard_map/jit(_where)/select_n | solution.py:286
  88.6 0.0 copy-done.2
  88.6 0.0 copy-done.3
  88.6 3.1 %fusion = f32[48,6528]{1,0:T(8,128)} fusion(bf16[48,512]{1,0:T(8,128)(2,1)S(1)} %copy-done.3, bf16[6528,512]{1,0:T(8,128)(2,1)S(1)} %copy-done.2), kind=kOutput, calls=%fused_computation.15 | convolution fusion | flops 320864256 | bytes 7987200 | tf_op jit(solution)/shard_map/bd,vd->bv/dot_general | solution.py:283
  91.7 0.0 copy-done.1
  (2 shorter events, 0.0 us)
Async XLA Ops:
  0.6 5.9 %copy-start = (bf16[448,512]{1,0:T(8,128)(2,1)S(1)}, bf16[448,512]{1,0:T(8,128)(2,1)}, u32[]{:S(2)}) copy-start(bf16[448,512]{1,0:T(8,128)(2,1)} %param.25) | copy-start | bytes 1376260
  12.5 64.3 %copy-start.4 = (s32[48]{0:T(128)S(1)}, s32[48]{0:T(128)}, u32[]{:S(2)}) copy-start(s32[48]{0:T(128)} %param.19) | copy-start | bytes 580
  76.8 11.8 %copy-start.2 = (bf16[6528,512]{1,0:T(8,128)(2,1)S(1)}, bf16[6528,512]{1,0:T(8,128)(2,1)}, u32[]{:S(2)}) copy-start(bf16[6528,512]{1,0:T(8,128)(2,1)} %param.24) | copy-start | bytes 20054020
  76.9 11.8 %copy-start.3 = (bf16[48,512]{1,0:T(8,128)(2,1)S(1)}, bf16[48,512]{1,0:T(8,128)(2,1)}, u32[]{:S(2)}) copy-start(bf16[48,512]{1,0:T(8,128)(2,1)} %get-tuple-element.6) | copy-start | bytes 147460
  76.9 14.9 %copy-start.1 = (bf16[448,512]{1,0:T(8,128)(2,1)S(1)}, bf16[448,512]{1,0:T(8,128)(2,1)}, u32[]{:S(2)}) copy-start(bf16[448,512]{1,0:T(8,128)(2,1)} %param.25) | copy-start | bytes 1376260

commit v2 on v1

v2 whole, which is shorter than its diff:
```python
import functools

import jax
import jax.numpy as jnp
from jax import lax
from jax.experimental import pallas as pl
from jax.experimental.pallas import tpu as pltpu
from jax.sharding import PartitionSpec as P

MESH = pl.DeviceIdType.MESH
GROUP = 16
LANES = 128
CHUNKS = 8
STEP_VMEM = 42 * 1024 * 1024
LAST_VMEM = 8 * 1024 * 1024
F32 = jnp.float32
BF16 = jnp.bfloat16
NT = (((1,), (1,)), ((), ()))


def dot_nt(a, b):
    return lax.dot_general(a, b, NT, preferred_element_type=F32)


def dot_nn(a, b):
    return jnp.dot(a, b, preferred_element_type=F32)


def layer_norm(x, gain, shift):
    mean = jnp.mean(x, axis=-1, keepdims=True)
    centred = x - mean
    variance = jnp.mean(centred * centred, axis=-1, keepdims=True)
    return (centred * lax.rsqrt(variance + 1e-5) * gain + shift).astype(BF16)


def step_kernel(
    n, tokens, positions, in_bias, out_bias, b_fc1, ln_layers, ln_final,
    embed, pos_table, w_qkv_hbm, w_cq_hbm, fc1_hbm, fc2_hbm, w_out, self_k, self_v, cross_k, cross_v,
    final_out, table, sk, sv,
    ck, cv, wo_full, pos_vmem, w_qkv, w_cq, fc1, fc2, emb_own, emb_partner, emb_chip, emb_slots, o_slots,
    rs_src, rs_slots, ag_slots, q_bd, scores, one_hot, columns,
    sem_e, sem_p, sem_own, sem_self, sem_cross, sem_w, pair_send, pair_recv, emb_send, emb_recv,
    o_send, o_recv, rs_send, rs_recv, ag_send, ag_recv, w_send, w_recv,
):
    layers, batch = sk.shape[0], sk.shape[1]
    head, ctx = sk.shape[2], sk.shape[3]
    width = table.shape[1]
    half, block = batch // 2, width // (n // 2)
    span = GROUP * head
    me = lax.axis_index("tp")
    core, chip = lax.rem(me, 2), lax.div(me, 2)
    partner = me + 1 - 2 * core

    def peer(k):
        return lax.rem(me + k, n)

    chunks = sem_e.shape[0]
    chunk = table.shape[0] // chunks
    table_loads = [pltpu.make_async_copy(embed.at[pl.ds(c * chunk, chunk)], table.at[pl.ds(c * chunk, chunk)], sem_e.at[c]) for c in range(chunks)]
    for c in table_loads:
        c.start()
    pos_load = pltpu.make_async_copy(pos_table, pos_vmem, sem_p)
    pos_load.start()
    own = [pltpu.make_async_copy(a, b, sem_own.at[i]) for i, (a, b) in enumerate(((w_qkv_hbm, w_qkv), (w_cq_hbm, w_cq), (fc1_hbm, fc1), (fc2_hbm, fc2)))]
    own[0].start()
    self_loads = [[pltpu.make_async_copy(a.at[l], b.at[l], sem_self.at[l, i]) for i, (a, b) in enumerate(((self_k, sk), (self_v, sv)))] for l in range(layers)]
    key_loads = [pltpu.make_async_copy(cross_k.at[l], ck.at[l], sem_cross.at[l, 0]) for l in range(layers)]
    val_loads = [pltpu.make_async_copy(cross_v.at[l], cv, sem_cross.at[l, 1]) for l in range(layers)]
    for c in self_loads[0]:
        c.start()
    for c in own[1:]:
        c.start()
    key_loads[0].start()
    val_loads[0].start()
    for l in range(1, layers):
        for c in self_loads[l]:
            c.start()
        key_loads[l].start()

    barrier = pltpu.get_barrier_semaphore()
    for k in range(1, n):
        pl.semaphore_signal(barrier, 1, device_id={"tp": peer(k)}, device_id_type=MESH)

    def remote(src, dst, send, recv, to):
        return pltpu.make_async_remote_copy(src, dst, send, recv, device_id={"tp": to}, device_id_type=MESH)

    order = sorted(range(1, n), key=lambda k: -min(k, n - k))

    def send_all(src_of, slots, send, recv):
        copies = [remote(src_of(peer(k)), slots.at[me], send.at[k], recv.at[me], peer(k)) for k in order]
        for c in copies:
            c.start()
        return copies

    def wait_all(copies, slots, send, recv):
        for k in order:
            j = peer(k)
            remote(slots.at[j], slots.at[j], send.at[k], recv.at[j], j).wait_recv()
        for c in copies:
            c.wait_send()

    parts = [(w_out.at[l, a], wo_full.at[l, a]) for l in range(layers) for a in range(2)]
    own_copies, first_hop, second_hop = {}, {}, {}

    def weights_start(i):
        src, full = parts[i]
        own_copies[i] = pltpu.make_async_copy(src, full.at[me], sem_w.at[i])
        own_copies[i].start()
        first_hop[i] = [remote(src, full.at[me], w_send.at[i, k], w_recv.at[i, me], peer(k)) for k in range(2, n, 2)]
        first_hop[i].append(remote(src, full.at[me], w_send.at[i, 1], w_recv.at[i, me], partner))
        for c in first_hop[i]:
            c.start()

    def weights_forward(i):
        src, full = parts[i]
        second_hop[i] = []
        for k in range(2, n, 2):
            j = peer(k)
            remote(src, full.at[j], w_send.at[i, k], w_recv.at[i, j], j).wait_recv()
            c = remote(full.at[j], full.at[j], w_send.at[i, k + 1], w_recv.at[i, j], partner)
            c.start()
            second_hop[i].append(c)

    def weights_wait(i):
        src, full = parts[i]
        remote(src, full.at[partner], w_send.at[i, 1], w_recv.at[i, partner], partner).wait_recv()
        for k in range(2, n, 2):
            j = lax.rem(partner + k, n)
            remote(src, full.at[j], w_send.at[i, k + 1], w_recv.at[i, j], partner).wait_recv()
        for c in first_hop[i] + second_hop[i]:
            c.wait_send()
        own_copies[i].wait()

    def as_column(row):
        i = lax.broadcasted_iota(jnp.int32, (batch, batch), 0)
        j = lax.broadcasted_iota(jnp.int32, (batch, batch), 1)
        return jnp.sum(jnp.where(i == j, jnp.broadcast_to(row.astype(F32), (batch, batch)), 0.0), axis=1, keepdims=True)

    token = as_column(tokens[...]).astype(jnp.int32) - me * table.shape[0]
    place = as_column(positions[...]).astype(jnp.int32)
    picked = jnp.zeros((batch, width), F32)
    for c in range(chunks):
        table_loads[c].wait()
        hit = lax.broadcasted_iota(jnp.int32, (batch, chunk), 1) + c * chunk == token
        picked = picked + dot_nn(jnp.where(hit, 1.0, 0.0).astype(BF16), table[c * chunk : (c + 1) * chunk])
    emb_own[...] = picked.astype(BF16)

    pl.semaphore_wait(barrier, n - 1)
    pair = remote(emb_own, emb_partner, pair_send, pair_recv, partner)
    pair.start()
    hit = lax.broadcasted_iota(jnp.int32, (batch, ctx), 1) == place
    hit = jnp.where(hit, 1.0, 0.0)
    for t in range(0, ctx, LANES):
        size = min(LANES, ctx - t)
        one_hot[t // LANES, :, :size] = hit[:, t : t + size]
    pos_load.wait()
    pos_rows = dot_nn(hit.astype(BF16), pos_vmem[...])
    pair.wait()
    pair_sum = picked + emb_partner[...].astype(F32)
    for r in range(2):
        emb_chip[r] = pair_sum[r * half : (r + 1) * half].astype(BF16)
    others = [k for k in order]
    sends = []
    for dc in (n // 4, *[d for d in range(1, n // 2) if d != n // 4]):
        for other in range(2):
            to = lax.rem(chip + dc, n // 2) * 2 + lax.rem(core + other, 2)
            sends.append(remote(emb_chip.at[core], emb_slots.at[chip, core], emb_send.at[dc, other], emb_recv.at[chip, core], to))
    for c in sends:
        c.start()
    weights_start(0)
    x_parts = [pair_sum[r * half : (r + 1) * half] for r in range(2)]
    for dc in range(1, n // 2):
        far = lax.rem(chip + dc, n // 2)
        for r in range(2):
            remote(emb_chip.at[0], emb_slots.at[far, r], emb_send.at[dc, r], emb_recv.at[far, r], far * 2 + r).wait_recv()
            x_parts[r] = x_parts[r] + emb_slots[far, r].astype(F32)
    for c in sends:
        c.wait_send()
    x = jnp.concatenate(x_parts, axis=0) + pos_rows

    row = lax.broadcasted_iota(jnp.int32, (batch, span), 0)
    col = lax.broadcasted_iota(jnp.int32, (batch, span), 1)
    diagonal = lax.rem(row, GROUP) == lax.div(col, head)
    group_diagonal = diagonal[:GROUP]

    def attend(q, keys, vals, finish):
        length = keys.shape[2]
        wide = jnp.concatenate([q] * GROUP, axis=1)
        q_bd[...] = jnp.where(diagonal, wide, 0).astype(BF16)
        for g in range(batch // GROUP):
            rows = slice(g * GROUP, (g + 1) * GROUP)
            scores[rows, :length] = dot_nn(q_bd[rows], keys[rows].reshape(span, length))
        weights, extra = finish(scores[:, :length] * (head ** -0.5))
        out = []
        for g in range(batch // GROUP):
            rows = slice(g * GROUP, (g + 1) * GROUP)
            full = dot_nt(weights[rows], vals[rows].reshape(span, length))
            full = jnp.where(group_diagonal, full, 0.0)
            while full.shape[1] > head:
                mid = full.shape[1] // 2
                full = full[:, :mid] + full[:, mid:]
            out.append(full)
        return jnp.concatenate(out, axis=0) + extra

    def exchange_heads(e, attended):
        slots, send, recv = o_slots.at[e], o_send.at[e], o_recv.at[e]
        slots[me] = jnp.concatenate([attended[:half], attended[half:]], axis=1).astype(BF16)
        return send_all(lambda j: slots.at[me], slots, send, recv)

    def gathered_heads(e, copies):
        slots, send, recv = o_slots.at[e], o_send.at[e], o_recv.at[e]
        wait_all(copies, slots, send, recv)
        got = [slots[j].astype(F32) for j in range(n)]
        sides = [jnp.concatenate([g[:, r * head : (r + 1) * head] for g in got], axis=1) for r in range(2)]
        return jnp.concatenate(sides, axis=0).astype(BF16)

    def put_columns(l, k_new, v_new):
        eye = (lax.broadcasted_iota(jnp.int32, (head, head), 0) == lax.broadcasted_iota(jnp.int32, (head, head), 1))
        eye = jnp.where(eye, 1.0, 0.0).astype(BF16)
        wide = batch * LANES
        spread = lax.broadcasted_iota(jnp.int32, (batch, wide), 0) == lax.div(lax.broadcasted_iota(jnp.int32, (batch, wide), 1), LANES)
        spread = jnp.where(spread, 1.0, 0.0).astype(BF16)
        for i, rows in enumerate((k_new, v_new)):
            columns[i] = dot_nn(dot_nt(eye, rows).astype(BF16), spread).astype(BF16)

        def one(b, carry):
            for t in range(0, ctx, LANES):
                size = min(LANES, ctx - t)
                here = jnp.broadcast_to(one_hot[t // LANES, pl.ds(b, 1), :], (head, LANES))[:, :size].astype(BF16) > 0.5
                for i, cache in enumerate((sk, sv)):
                    fresh = columns[i, :, pl.ds(pl.multiple_of(b * LANES, LANES), LANES)][:, :size]
                    cache[l, b, :, t : t + size] = jnp.where(here, fresh, cache[l, b, :, t : t + size])
            return carry

        lax.fori_loop(0, batch, one, 0)

    for l in range(layers):
        ln = ln_layers[l]
        h = layer_norm(x, ln[0, 0:1], ln[0, 1:2])
        if l == 0:
            own[0].wait()
        q = (dot_nt(h, w_qkv[l, 0]) + in_bias[l, 0]).astype(BF16)
        k_new = dot_nt(h, w_qkv[l, 1]).astype(BF16)
        v_new = (dot_nt(h, w_qkv[l, 2]) + in_bias[l, 1]).astype(BF16)
        for c in self_loads[l]:
            c.wait()
        new_score = jnp.sum(q.astype(F32) * k_new.astype(F32), axis=-1, keepdims=True) * (head ** -0.5)

        def finish_self(s):
            s = jnp.where(lax.broadcasted_iota(jnp.int32, s.shape, 1) < place, s, -1e30)
            peak = jnp.maximum(jnp.max(s, axis=-1, keepdims=True), new_score)
            e = jnp.exp(s - peak)
            e_new = jnp.exp(new_score - peak)
            total = jnp.sum(e, axis=-1, keepdims=True) + e_new
            return (e / total).astype(BF16), (e_new / total).astype(BF16).astype(F32) * v_new.astype(F32)

        def finish_cross(s):
            e = jnp.exp(s - jnp.max(s, axis=-1, keepdims=True))
            return (e / jnp.sum(e, axis=-1, keepdims=True)).astype(BF16), 0.0

        attended = attend(q, sk.at[l], sv.at[l], finish_self)
        copies = exchange_heads(2 * l, attended)
        weights_start(2 * l + 1)
        weights_forward(2 * l)
        put_columns(l, k_new, v_new)
        weights_wait(2 * l)
        heads = gathered_heads(2 * l, copies)
        x = x + dot_nn(heads, wo_full[l, 0].reshape(n * head, width)).astype(BF16).astype(F32) + out_bias[0, l : l + 1]

        h = layer_norm(x, ln[1, 0:1], ln[1, 1:2])
        if l == 0:
            for c in own[1:]:
                c.wait()
        q = (dot_nt(h, w_cq[l]) + in_bias[l, 2]).astype(BF16)
        key_loads[l].wait()
        val_loads[l].wait()
        attended = attend(q, ck.at[l], cv, finish_cross)
        copies = exchange_heads(2 * l + 1, attended)
        weights_forward(2 * l + 1)
        weights_wait(2 * l + 1)
        if l + 1 < layers:
            val_loads[l + 1].start()
        heads = gathered_heads(2 * l + 1, copies)
        x = x + dot_nn(heads, wo_full[l, 1].reshape(n * head, width)).astype(BF16).astype(F32) + out_bias[1, l : l + 1]

        h = layer_norm(x, ln[2, 0:1], ln[2, 1:2])
        hidden = dot_nn(h, fc1[l]) + b_fc1[l : l + 1]
        active = (0.5 * hidden * (1.0 + lax.erf(hidden * (0.5 ** 0.5)))).astype(BF16)
        partial = dot_nn(active, fc2[l])
        for j in range(n):
            r, c = j // (n // 2), j % (n // 2)
            rs_src[l, j] = partial[r * half : (r + 1) * half, c * block : (c + 1) * block]
        copies = send_all(lambda j: rs_src.at[l, j], rs_slots.at[l], rs_send.at[l], rs_recv.at[l])
        rs_slots[l, me] = rs_src[l, me]
        if l + 1 < layers:
            weights_start(2 * l + 2)
        wait_all(copies, rs_slots.at[l], rs_send.at[l], rs_recv.at[l])
        total = rs_slots[l, 0]
        for j in range(1, n):
            total = total + rs_slots[l, j]
        ag_slots[l, me] = total.astype(BF16)
        copies = send_all(lambda j: ag_slots.at[l, me], ag_slots.at[l], ag_send.at[l], ag_recv.at[l])
        wait_all(copies, ag_slots.at[l], ag_send.at[l], ag_recv.at[l])
        sides = [jnp.concatenate([ag_slots[l, r * (n // 2) + c].astype(F32) for c in range(n // 2)], axis=1) for r in range(2)]
        x = x + jnp.concatenate(sides, axis=0) + out_bias[2, l : l + 1]

    final_out[...] = layer_norm(x, ln_final[0:1], ln_final[1:2])


def last_kernel(final, table, sk, sv, logits_out, keys_out, vals_out, logits, sems, logit_sems):
    copies = []
    for i, (src, dst) in enumerate(((sk, keys_out), (sv, vals_out))):
        for l in range(sk.shape[0]):
            copies.append(pltpu.make_async_copy(src.at[l], dst.at[l], sems.at[i, l]))
            copies[-1].start()
    h = final[...]
    pieces = logit_sems.shape[0]
    piece = logits.shape[1] // pieces
    for c in range(pieces):
        here = pl.ds(c * piece, piece)
        logits[:, here] = dot_nt(h, table[here, :])
        copies.append(pltpu.make_async_copy(logits.at[:, here], logits_out.at[:, here], logit_sems.at[c]))
        copies[-1].start()
    for c in copies:
        c.wait()


def solution(mesh):
    n = mesh.shape["tp"]

    def local_step(tokens, positions, self_keys, self_vals, cross_keys, cross_vals, embed_table, pos_table, w_qkv, w_cq, in_bias, w_out, out_bias, w_fc1, b_fc1, w_fc2, ln_layers, ln_final):
        layers, batch, ctx, _, head = self_keys.shape
        frames = cross_keys.shape[2]
        shard_rows, width = embed_table.shape
        hidden = w_fc1.shape[2]
        half, block = batch // 2, width // (n // 2)

        def by_place(cache):
            return jnp.transpose(cache[:, :, :, 0, :], (0, 1, 3, 2))

        vmem = pl.BlockSpec(memory_space=pltpu.VMEM)
        hbm = pl.BlockSpec(memory_space=pl.ANY)
        sem = pltpu.SemaphoreType.DMA
        cache_rows = (layers, batch, head, ctx)
        final_hidden, table, sk, sv = pl.pallas_call(
            functools.partial(step_kernel, n),
            out_shape=(pltpu.VMEM((batch, width), BF16), pltpu.VMEM((shard_rows, width), BF16), pltpu.VMEM(cache_rows, BF16), pltpu.VMEM(cache_rows, BF16)),
            in_specs=[vmem] * 7 + [hbm] * 11,
            out_specs=(vmem, vmem, vmem, vmem),
            scratch_shapes=[
                pltpu.VMEM((layers, batch, head, frames), BF16),
                pltpu.VMEM((batch, head, frames), BF16),
                pltpu.VMEM((layers, 2, n, head, width), BF16),
                pltpu.VMEM(pos_table.shape, BF16),
                pltpu.VMEM((layers, 3, head, width), BF16),
                pltpu.VMEM((layers, head, width), BF16),
                pltpu.VMEM(w_fc1.shape, BF16),
                pltpu.VMEM(w_fc2.shape, BF16),
                pltpu.VMEM((batch, width), BF16),
                pltpu.VMEM((batch, width), BF16),
                pltpu.VMEM((2, half, width), BF16),
                pltpu.VMEM((n // 2, 2, half, width), BF16),
                pltpu.VMEM((2 * layers, n, half, 2 * head), BF16),
                pltpu.VMEM((layers, n, half, block), F32),
                pltpu.VMEM((layers, n, half, block), F32),
                pltpu.VMEM((layers, n, half, block), BF16),
                pltpu.VMEM((batch, GROUP * head), BF16),
                pltpu.VMEM((batch, frames), F32),
                pltpu.VMEM((pl.cdiv(ctx, LANES), batch, LANES), F32),
                pltpu.VMEM((2, head, batch * LANES), BF16),
                sem((CHUNKS,)), sem, sem((4,)), sem((layers, 2)), sem((layers, 2)), sem((2 * layers,)),
                sem, sem, sem((n // 2, 2)), sem((n // 2, 2)),
                sem((2 * layers, n)), sem((2 * layers, n)), sem((layers, n)), sem((layers, n)), sem((layers, n)), sem((layers, n)),
                sem((2 * layers, n)), sem((2 * layers, n)),
            ],
            compiler_params=pltpu.CompilerParams(collective_id=0, has_side_effects=True, vmem_limit_bytes=STEP_VMEM),
            name="decode_step",
        )(
            tokens[None], positions[None], in_bias, jnp.transpose(out_bias, (1, 0, 2)), b_fc1, ln_layers, ln_final,
            embed_table, pos_table, jnp.transpose(w_qkv[:, :, :, 0, :], (0, 2, 3, 1)), jnp.transpose(w_cq[:, :, 0, :], (0, 2, 1)),
            w_fc1, w_fc2, w_out[:, :, 0],
            by_place(self_keys), by_place(self_vals), by_place(cross_keys), by_place(cross_vals),
        )

        def in_vmem(a):
            return pltpu.with_memory_space_constraint(a, pltpu.VMEM)

        logits, new_keys, new_vals = pl.pallas_call(
            last_kernel,
            out_shape=(jax.ShapeDtypeStruct((batch, shard_rows), F32), jax.ShapeDtypeStruct(cache_rows, BF16), jax.ShapeDtypeStruct(cache_rows, BF16)),
            in_specs=[vmem] * 4,
            out_specs=(hbm, hbm, hbm),
            scratch_shapes=[pltpu.VMEM((batch, shard_rows), F32), sem((2, layers)), sem((3,))],
            compiler_params=pltpu.CompilerParams(vmem_limit_bytes=LAST_VMEM),
            name="last",
        )(in_vmem(final_hidden), in_vmem(table), in_vmem(sk), in_vmem(sv))

        def as_given(cache):
            return jnp.transpose(cache, (0, 1, 3, 2))[:, :, :, None, :]

        return logits, as_given(new_keys), as_given(new_vals)

    batch_spec = P("dp")
    cache_spec = P(None, "dp", None, "tp", None)
    in_specs = (batch_spec, batch_spec, cache_spec, cache_spec, cache_spec, cache_spec, P("tp", None), P(None, None), P(None, None, None, "tp", None), P(None, None, "tp", None), P(None, None, "tp", None), P(None, None, "tp", None, None), P(None, None, None), P(None, None, "tp"), P(None, "tp"), P(None, "tp", None), P(None, None, None, None), P(None, None))
    out_specs = (P("dp", "tp"), cache_spec, cache_spec)
    return jax.shard_map(local_step, mesh=mesh, in_specs=in_specs, out_specs=out_specs, check_vma=False)
```

time: 92 us -> 72.9 us (0.79)
  other arithmetic: 14.6 us -> 0 us
  local copies, waits for them, and re-layouts: 9.07 us -> 0 us
  Pallas kernels: 64.2 us -> 72.1 us
  matrix products: 3.13 us -> 0 us
    select_n x3 -> x0, other arithmetic: 13.1 us -> none  [the longest x1 11.7 us: local_step(): new_vals = jnp.where(write_mask, v_new[:, :, None, None, :], self_vals)]
    pallas_call x1 -> x2, Pallas kernels: 64.2 us -> 72.1 us  [the longest x1 67.1 us: local_step(): pl.pallas_call(functools.partial(step_kernel, n), out_shape=(pltpu.VMEM((...]
    gather x2 -> x0, local copies, waits for them, and re-layouts: 5.09 us -> none  [the longest x1 4.43 us: local_step(): jnp.take(embed_table, jnp.clip(local_ids, 0, shard_rows - 1), axis=0)]
    dot_general x1 -> x0, matrix products: 3.13 us -> none  [local_step(): jnp.einsum('bd,vd->bv', final_hidden, embed_table, preferred_element_type...]
    unnamed x12 -> x0, local copies, waits for them, and re-layouts: 2.03 us -> none
    and x2 -> x0, other arithmetic: 1.38 us -> none  [the longest x1 0.72 us: local_step(): jnp.take(embed_table, jnp.clip(local_ids, 0, shard_rows - 1), axis=0)]
    broadcast_in_dim x1 -> x0, local copies, waits for them, and re-layouts: 1.35 us -> none  [local_step(): positions[:, None]]
where the time goes in v2:
time: 72.9 us; the launch traced here: 72.8 us
  Pallas kernels  72.1 us (99%)
    pallas_call x1, Pallas kernels, local_step(): pl.pallas_call(functools.partial(step_kernel, n), out_shape=(pltpu.VMEM((...  67.1 us
    pallas_call x1, Pallas kernels, local_step(): pl.pallas_call(last_kernel, out_shape=(jax.ShapeDtypeStruct((batch, shard...  5.05 us

profile of v2, /device:TPU:113, one launch (start us, length us, event | category | flops | bytes accessed | tf_op | source)
XLA Modules:
  0.0 72.8 jit_solution(12631573518784240943)
XLA Ops:
  0.6 67.1 %decode_step.1 = (bf16[48,512]{1,0:T(8,128)(2,1)S(1)}, bf16[6528,512]{1,0:T(8,128)(2,1)S(1)}, bf16[2,48,64,448]{3,2,1,0:T(8,128)(2,1)S(1)}, bf16[2,48,64,448]{3,2,1,0:T(8,128)(2,1)S(1)}) custom-call(s32[1,48]{1,0:T(1,128)} %bitcast.40, s32[1,48]{1,0:T(1,128)} %bitcast.41, f32[2,3,1,64]{3,2,1,0:T(1,128)} %in_bias.1, f32[3,2,512]{2,1,0:T(2,128)} %bitcast.39, ...), custom_call_target="tpu_custom_call" | custom-call | tf_op jit(solution)/shard_map/decode_step/pallas_call | solution.py:345
  67.7 5.0 %last.1 = (f32[48,6528]{1,0:T(8,128)}, bf16[2,48,64,448]{3,2,1,0:T(8,128)(2,1)}, bf16[2,48,64,448]{3,2,1,0:T(8,128)(2,1)}) custom-call(bf16[48,512]{1,0:T(8,128)(2,1)S(1)} %get-tuple-element.10.final, bf16[6528,512]{1,0:T(8,128)(2,1)S(1)} %get-tuple-element.11.table, bf16[2,48,64,448]{3,2,1,0:T(8,128)(2,1)S(1)} %get-tuple-element.12.sk, ...), custom_call_target="tpu_custom_call" | custom-call | tf_op jit(solution)/shard_map/last/pallas_call | solution.py:388

commit v3 on v2

--- a/solution.py
+++ b/solution.py
@@ -8,7 +8,6 @@
 from jax.sharding import PartitionSpec as P
 
 MESH = pl.DeviceIdType.MESH
-GROUP = 16
 LANES = 128
 CHUNKS = 8
 STEP_VMEM = 42 * 1024 * 1024
@@ -38,7 +37,7 @@
     embed, pos_table, w_qkv_hbm, w_cq_hbm, fc1_hbm, fc2_hbm, w_out, self_k, self_v, cross_k, cross_v,
     final_out, table, sk, sv,
     ck, cv, wo_full, pos_vmem, w_qkv, w_cq, fc1, fc2, emb_own, emb_partner, emb_chip, emb_slots, o_slots,
-    rs_src, rs_slots, ag_slots, q_bd, scores, one_hot, columns,
+    rs_src, rs_slots, ag_slots, one_hot, columns, x, places, fresh,
     sem_e, sem_p, sem_own, sem_self, sem_cross, sem_w, pair_send, pair_recv, emb_send, emb_recv,
     o_send, o_recv, rs_send, rs_recv, ag_send, ag_recv, w_send, w_recv,
 ):
@@ -46,13 +45,17 @@
     head, ctx = sk.shape[2], sk.shape[3]
     width = table.shape[1]
     half, block = batch // 2, width // (n // 2)
-    span = GROUP * head
+    span = half * head
     me = lax.axis_index("tp")
     core, chip = lax.rem(me, 2), lax.div(me, 2)
     partner = me + 1 - 2 * core
 
     def peer(k):
         return lax.rem(me + k, n)
+
+    barrier = pltpu.get_barrier_semaphore()
+    for k in range(1, n):
+        pl.semaphore_signal(barrier, 1, device_id={"tp": peer(k)}, device_id_type=MESH)
 
     chunks = sem_e.shape[0]
     chunk = table.shape[0] // chunks
@@ -62,24 +65,10 @@
     pos_load = pltpu.make_async_copy(pos_table, pos_vmem, sem_p)
     pos_load.start()
     own = [pltpu.make_async_copy(a, b, sem_own.at[i]) for i, (a, b) in enumerate(((w_qkv_hbm, w_qkv), (w_cq_hbm, w_cq), (fc1_hbm, fc1), (fc2_hbm, fc2)))]
-    own[0].start()
     self_loads = [[pltpu.make_async_copy(a.at[l], b.at[l], sem_self.at[l, i]) for i, (a, b) in enumerate(((self_k, sk), (self_v, sv)))] for l in range(layers)]
     key_loads = [pltpu.make_async_copy(cross_k.at[l], ck.at[l], sem_cross.at[l, 0]) for l in range(layers)]
     val_loads = [pltpu.make_async_copy(cross_v.at[l], cv, sem_cross.at[l, 1]) for l in range(layers)]
-    for c in self_loads[0]:
-        c.start()
-    for c in own[1:]:
-        c.start()
-    key_loads[0].start()
-    val_loads[0].start()
-    for l in range(1, layers):
-        for c in self_loads[l]:
-            c.start()
-        key_loads[l].start()
-
-    barrier = pltpu.get_barrier_semaphore()
-    for k in range(1, n):
-        pl.semaphore_signal(barrier, 1, device_id={"tp": peer(k)}, device_id_type=MESH)
+    later_loads = [own[0], *self_loads[0], *own[1:], key_loads[0], val_loads[0]]
 
     def remote(src, dst, send, recv, to):
         return pltpu.make_async_remote_copy(src, dst, send, recv, device_id={"tp": to}, device_id_type=MESH)
@@ -87,17 +76,15 @@
     order = sorted(range(1, n), key=lambda k: -min(k, n - k))
 
     def send_all(src_of, slots, send, recv):
-        copies = [remote(src_of(peer(k)), slots.at[me], send.at[k], recv.at[me], peer(k)) for k in order]
-        for c in copies:
-            c.start()
-        return copies
-
-    def wait_all(copies, slots, send, recv):
+        for k in order:
+            remote(src_of(peer(k)), slots.at[me], send.at[k], recv.at[me], peer(k)).start()
+
+    def wait_all(slots, send, recv):
         for k in order:
             j = peer(k)
             remote(slots.at[j], slots.at[j], send.at[k], recv.at[j], j).wait_recv()
-        for c in copies:
-            c.wait_send()
+        for k in order:
+            remote(slots.at[me], slots.at[me], send.at[k], recv.at[me], peer(k)).wait_send()
 
     parts = [(w_out.at[l, a], wo_full.at[l, a]) for l in range(layers) for a in range(2)]
     own_copies, first_hop, second_hop = {}, {}, {}
@@ -138,14 +125,17 @@
 
     token = as_column(tokens[...]).astype(jnp.int32) - me * table.shape[0]
     place = as_column(positions[...]).astype(jnp.int32)
+    pl.semaphore_wait(barrier, n - 1)
+    weights_start(0)
     picked = jnp.zeros((batch, width), F32)
     for c in range(chunks):
         table_loads[c].wait()
         hit = lax.broadcasted_iota(jnp.int32, (batch, chunk), 1) + c * chunk == token
         picked = picked + dot_nn(jnp.where(hit, 1.0, 0.0).astype(BF16), table[c * chunk : (c + 1) * chunk])
+    for c in later_loads:
+        c.start()
     emb_own[...] = picked.astype(BF16)
 
-    pl.semaphore_wait(barrier, n - 1)
     pair = remote(emb_own, emb_partner, pair_send, pair_recv, partner)
     pair.start()
     hit = lax.broadcasted_iota(jnp.int32, (batch, ctx), 1) == place
@@ -167,7 +157,7 @@
             sends.append(remote(emb_chip.at[core], emb_slots.at[chip, core], emb_send.at[dc, other], emb_recv.at[chip, core], to))
     for c in sends:
         c.start()
-    weights_start(0)
+    weights_start(1)
     x_parts = [pair_sum[r * half : (r + 1) * half] for r in range(2)]
     for dc in range(1, n // 2):
         far = lax.rem(chip + dc, n // 2)
@@ -176,51 +166,50 @@
             x_parts[r] = x_parts[r] + emb_slots[far, r].astype(F32)
     for c in sends:
         c.wait_send()
-    x = jnp.concatenate(x_parts, axis=0) + pos_rows
-
-    row = lax.broadcasted_iota(jnp.int32, (batch, span), 0)
-    col = lax.broadcasted_iota(jnp.int32, (batch, span), 1)
-    diagonal = lax.rem(row, GROUP) == lax.div(col, head)
-    group_diagonal = diagonal[:GROUP]
+    for r in range(2):
+        x[r] = x_parts[r] + pos_rows[r * half : (r + 1) * half]
+        places[r] = jnp.broadcast_to(place[r * half : (r + 1) * half], (half, LANES))
+
+    diagonal = lax.broadcasted_iota(jnp.int32, (half, span), 0) == lax.div(lax.broadcasted_iota(jnp.int32, (half, span), 1), head)
 
     def attend(q, keys, vals, finish):
         length = keys.shape[2]
-        wide = jnp.concatenate([q] * GROUP, axis=1)
-        q_bd[...] = jnp.where(diagonal, wide, 0).astype(BF16)
-        for g in range(batch // GROUP):
-            rows = slice(g * GROUP, (g + 1) * GROUP)
-            scores[rows, :length] = dot_nn(q_bd[rows], keys[rows].reshape(span, length))
-        weights, extra = finish(scores[:, :length] * (head ** -0.5))
-        out = []
-        for g in range(batch // GROUP):
-            rows = slice(g * GROUP, (g + 1) * GROUP)
-            full = dot_nt(weights[rows], vals[rows].reshape(span, length))
-            full = jnp.where(group_diagonal, full, 0.0)
-            while full.shape[1] > head:
-                mid = full.shape[1] // 2
-                full = full[:, :mid] + full[:, mid:]
-            out.append(full)
-        return jnp.concatenate(out, axis=0) + extra
-
-    def exchange_heads(e, attended):
-        slots, send, recv = o_slots.at[e], o_send.at[e], o_recv.at[e]
-        slots[me] = jnp.concatenate([attended[:half], attended[half:]], axis=1).astype(BF16)
-        return send_all(lambda j: slots.at[me], slots, send, recv)
-
-    def gathered_heads(e, copies):
-        slots, send, recv = o_slots.at[e], o_send.at[e], o_recv.at[e]
-        wait_all(copies, slots, send, recv)
-        got = [slots[j].astype(F32) for j in range(n)]
-        sides = [jnp.concatenate([g[:, r * head : (r + 1) * head] for g in got], axis=1) for r in range(2)]
-        return jnp.concatenate(sides, axis=0).astype(BF16)
-
-    def put_columns(l, k_new, v_new):
+        wide = jnp.where(diagonal, jnp.concatenate([q] * half, axis=1), 0).astype(BF16)
+        scores = dot_nn(wide, keys[...].reshape(span, length))
+        weights, extra = finish(scores * (head ** -0.5))
+        full = jnp.where(diagonal, dot_nt(weights, vals[...].reshape(span, length)), 0.0)
+        total = full[:, :LANES]
+        for c in range(LANES, span, LANES):
+            total = total + full[:, c : c + LANES]
+        out = total[:, :head]
+        for c in range(head, LANES, head):
+            out = out + total[:, c : c + head]
+        return out + extra
+
+    def head_slots(e, r):
+        return o_slots.at[e, r], o_send.at[e, r], o_recv.at[e, r]
+
+    def exchange_heads(e, r, attended):
+        slots, send, recv = head_slots(e, r)
+        slots[me] = attended.astype(BF16)
+        send_all(lambda j: slots.at[me], slots, send, recv)
+
+    def gathered_heads(e, r):
+        slots, send, recv = head_slots(e, r)
+        wait_all(slots, send, recv)
+        return jnp.concatenate([slots[j].astype(F32) for j in range(n)], axis=1).astype(BF16)
+
+    def project(l, a, heads):
+        return dot_nn(heads, wo_full[l, a].reshape(n * head, width)).astype(BF16).astype(F32)
+
+    def put_columns(l):
         eye = (lax.broadcasted_iota(jnp.int32, (head, head), 0) == lax.broadcasted_iota(jnp.int32, (head, head), 1))
         eye = jnp.where(eye, 1.0, 0.0).astype(BF16)
         wide = batch * LANES
         spread = lax.broadcasted_iota(jnp.int32, (batch, wide), 0) == lax.div(lax.broadcasted_iota(jnp.int32, (batch, wide), 1), LANES)
         spread = jnp.where(spread, 1.0, 0.0).astype(BF16)
-        for i, rows in enumerate((k_new, v_new)):
+        for i in range(2):
+            rows = jnp.concatenate([fresh[i, 0], fresh[i, 1]], axis=0).astype(BF16)
             columns[i] = dot_nn(dot_nt(eye, rows).astype(BF16), spread).astype(BF16)
 
         def one(b, carry):
@@ -234,77 +223,128 @@
 
         lax.fori_loop(0, batch, one, 0)
 
-    for l in range(layers):
+    def self_stage(l, r):
         ln = ln_layers[l]
-        h = layer_norm(x, ln[0, 0:1], ln[0, 1:2])
-        if l == 0:
-            own[0].wait()
+        rows = pl.ds(r * half, half)
+        h = layer_norm(x[r], ln[0, 0:1], ln[0, 1:2])
         q = (dot_nt(h, w_qkv[l, 0]) + in_bias[l, 0]).astype(BF16)
         k_new = dot_nt(h, w_qkv[l, 1]).astype(BF16)
         v_new = (dot_nt(h, w_qkv[l, 2]) + in_bias[l, 1]).astype(BF16)
-        for c in self_loads[l]:
-            c.wait()
+        fresh[0, r] = k_new.astype(F32)
+        fresh[1, r] = v_new.astype(F32)
+        here = places[r][:, :1]
         new_score = jnp.sum(q.astype(F32) * k_new.astype(F32), axis=-1, keepdims=True) * (head ** -0.5)
 
-        def finish_self(s):
-            s = jnp.where(lax.broadcasted_iota(jnp.int32, s.shape, 1) < place, s, -1e30)
+        def finish(s):
+            s = jnp.where(lax.broadcasted_iota(jnp.int32, s.shape, 1) < here, s, -1e30)
             peak = jnp.maximum(jnp.max(s, axis=-1, keepdims=True), new_score)
             e = jnp.exp(s - peak)
             e_new = jnp.exp(new_score - peak)
             total = jnp.sum(e, axis=-1, keepdims=True) + e_new
             return (e / total).astype(BF16), (e_new / total).astype(BF16).astype(F32) * v_new.astype(F32)
 
-        def finish_cross(s):
+        attended = attend(q, sk.at[l, rows], sv.at[l, rows], finish)
+        exchange_heads(2 * l, r, attended)
+
+    def cross_stage(l, r):
+        ln = ln_layers[l]
+        rows = pl.ds(r * half, half)
+        x[r] = x[r] + project(l, 0, gathered_heads(2 * l, r)) + out_bias[0, l : l + 1]
+        h = layer_norm(x[r], ln[1, 0:1], ln[1, 1:2])
+        q = (dot_nt(h, w_cq[l]) + in_bias[l, 2]).astype(BF16)
+
+        def finish(s):
             e = jnp.exp(s - jnp.max(s, axis=-1, keepdims=True))
             return (e / jnp.sum(e, axis=-1, keepdims=True)).astype(BF16), 0.0
 
-        attended = attend(q, sk.at[l], sv.at[l], finish_self)
-        copies = exchange_heads(2 * l, attended)
-        weights_start(2 * l + 1)
-        weights_forward(2 * l)
-        put_columns(l, k_new, v_new)
-        weights_wait(2 * l)
-        heads = gathered_heads(2 * l, copies)
-        x = x + dot_nn(heads, wo_full[l, 0].reshape(n * head, width)).astype(BF16).astype(F32) + out_bias[0, l : l + 1]
-
-        h = layer_norm(x, ln[1, 0:1], ln[1, 1:2])
-        if l == 0:
-            for c in own[1:]:
-                c.wait()
-        q = (dot_nt(h, w_cq[l]) + in_bias[l, 2]).astype(BF16)
-        key_loads[l].wait()
-        val_loads[l].wait()
-        attended = attend(q, ck.at[l], cv, finish_cross)
-        copies = exchange_heads(2 * l + 1, attended)
-        weights_forward(2 * l + 1)
-        weights_wait(2 * l + 1)
-        if l + 1 < layers:
-            val_loads[l + 1].start()
-        heads = gathered_heads(2 * l + 1, copies)
-        x = x + dot_nn(heads, wo_full[l, 1].reshape(n * head, width)).astype(BF16).astype(F32) + out_bias[1, l : l + 1]
-
-        h = layer_norm(x, ln[2, 0:1], ln[2, 1:2])
+        attended = attend(q, ck.at[l, rows], cv.at[rows], finish)
+        exchange_heads(2 * l + 1, r, attended)
+
+    def mlp_stage(l, r):
+        ln = ln_layers[l]
+        x[r] = x[r] + project(l, 1, gathered_heads(2 * l + 1, r)) + out_bias[1, l : l + 1]
+        h = layer_norm(x[r], ln[2, 0:1], ln[2, 1:2])
         hidden = dot_nn(h, fc1[l]) + b_fc1[l : l + 1]
         active = (0.5 * hidden * (1.0 + lax.erf(hidden * (0.5 ** 0.5)))).astype(BF16)
         partial = dot_nn(active, fc2[l])
-        for j in range(n):
-            r, c = j // (n // 2), j % (n // 2)
-            rs_src[l, j] = partial[r * half : (r + 1) * half, c * block : (c + 1) * block]
-        copies = send_all(lambda j: rs_src.at[l, j], rs_slots.at[l], rs_send.at[l], rs_recv.at[l])
+        for c in range(n // 2):
+            rs_src[l, r * (n // 2) + c] = partial[:, c * block : (c + 1) * block]
+        for k in order:
+            pl.when(lax.div(peer(k), n // 2) == r)(rs_copy(l, k).start)
+
+    def rs_copy(l, k):
+        j = peer(k)
+        return remote(rs_src.at[l, j], rs_slots.at[l, me], rs_send.at[l, k], rs_recv.at[l, me], j)
+
+    def sum_stage(l):
+        wait_all(rs_slots.at[l], rs_send.at[l], rs_recv.at[l])
         rs_slots[l, me] = rs_src[l, me]
-        if l + 1 < layers:
-            weights_start(2 * l + 2)
-        wait_all(copies, rs_slots.at[l], rs_send.at[l], rs_recv.at[l])
         total = rs_slots[l, 0]
         for j in range(1, n):
             total = total + rs_slots[l, j]
         ag_slots[l, me] = total.astype(BF16)
-        copies = send_all(lambda j: ag_slots.at[l, me], ag_slots.at[l], ag_send.at[l], ag_recv.at[l])
-        wait_all(copies, ag_slots.at[l], ag_send.at[l], ag_recv.at[l])
-        sides = [jnp.concatenate([ag_slots[l, r * (n // 2) + c].astype(F32) for c in range(n // 2)], axis=1) for r in range(2)]
-        x = x + jnp.concatenate(sides, axis=0) + out_bias[2, l : l + 1]
-
-    final_out[...] = layer_norm(x, ln_final[0:1], ln_final[1:2])
+        send_all(lambda j: ag_slots.at[l, me], ag_slots.at[l], ag_send.at[l], ag_recv.at[l])
+
+    def add_stage(l, r):
+        for k in order:
+            j = peer(k)
+            slot = ag_slots.at[l, j]
+            pl.when(lax.div(j, n // 2) == r)(remote(slot, slot, ag_send.at[l, k], ag_recv.at[l, j], j).wait_recv)
+        x[r] = x[r] + jnp.concatenate([ag_slots[l, r * (n // 2) + c].astype(F32) for c in range(n // 2)], axis=1) + out_bias[2, l : l + 1]
+
+    def both(stage, l):
+        def one(r, carry):
+            stage(l, r)
+            return carry
+
+        lax.fori_loop(0, 2, one, 0)
+
+    def sent(l):
+        for k in order:
+            remote(ag_slots.at[l, me], ag_slots.at[l, me], ag_send.at[l, k], ag_recv.at[l, me], peer(k)).wait_send()
+
+    def next_stage(l, r):
+        add_stage(l - 1, r)
+        self_stage(l, r)
+
+    def end_stage(l, r):
+        add_stage(l - 1, r)
+        final_out[pl.ds(pl.multiple_of(r * half, half), half)] = layer_norm(x[r], ln_final[0:1], ln_final[1:2])
+
+    own[0].wait()
+    for c in self_loads[0]:
+        c.wait()
+    both(self_stage, 0)
+    for l in range(layers):
+        last = l + 1 == layers
+        weights_forward(2 * l)
+        if l == 0:
+            for c in own[1:]:
+                c.wait()
+        weights_wait(2 * l)
+        key_loads[l].wait()
+        val_loads[l].wait()
+        if not last:
+            for c in (*self_loads[l + 1], key_loads[l + 1]):
+                c.start()
+        both(cross_stage, l)
+        if not last:
+            val_loads[l + 1].start()
+            weights_start(2 * l + 2)
+        weights_forward(2 * l + 1)
+        weights_wait(2 * l + 1)
+        both(mlp_stage, l)
+        if not last:
+            weights_start(2 * l + 3)
+        put_columns(l)
+        sum_stage(l)
+        if not last:
+            for c in self_loads[l + 1]:
+                c.wait()
+            both(next_stage, l + 1)
+        else:
+            both(end_stage, l + 1)
+        sent(l)
 
 
 def last_kernel(final, table, sk, sv, logits_out, keys_out, vals_out, logits, sems, logit_sems):
@@ -360,17 +400,18 @@
                 pltpu.VMEM((batch, width), BF16),
                 pltpu.VMEM((2, half, width), BF16),
                 pltpu.VMEM((n // 2, 2, half, width), BF16),
-                pltpu.VMEM((2 * layers, n, half, 2 * head), BF16),
+                pltpu.VMEM((2 * layers, 2, n, half, head), BF16),
                 pltpu.VMEM((layers, n, half, block), F32),
                 pltpu.VMEM((layers, n, half, block), F32),
                 pltpu.VMEM((layers, n, half, block), BF16),
-                pltpu.VMEM((batch, GROUP * head), BF16),
-                pltpu.VMEM((batch, frames), F32),
                 pltpu.VMEM((pl.cdiv(ctx, LANES), batch, LANES), F32),
                 pltpu.VMEM((2, head, batch * LANES), BF16),
+                pltpu.VMEM((2, half, width), F32),
+                pltpu.VMEM((2, half, LANES), jnp.int32),
+                pltpu.VMEM((2, 2, half, head), F32),
                 sem((CHUNKS,)), sem, sem((4,)), sem((layers, 2)), sem((layers, 2)), sem((2 * layers,)),
                 sem, sem, sem((n // 2, 2)), sem((n // 2, 2)),
-                sem((2 * layers, n)), sem((2 * layers, n)), sem((layers, n)), sem((layers, n)), sem((layers, n)), sem((layers, n)),
+                sem((2 * layers, 2, n)), sem((2 * layers, 2, n)), sem((layers, n)), sem((layers, n)), sem((layers, n)), sem((layers, n)),
                 sem((2 * layers, n)), sem((2 * layers, n)),
             ],
             compiler_params=pltpu.CompilerParams(collective_id=0, has_side_effects=True, vmem_limit_bytes=STEP_VMEM),

time: 72.9 us -> 65 us (0.89)
  Pallas kernels: 72.1 us -> 64.2 us
    pallas_call x1, Pallas kernels: 67.1 us -> 59.2 us  [local_step(): pl.pallas_call(functools.partial(step_kernel, n), out_shape=(pltpu.VMEM((...]
where the time goes in v3:
time: 65 us; the launch traced here: 64.9 us
  Pallas kernels  64.2 us (99%)
  between operations  0.65 us (1%)
    pallas_call x1, Pallas kernels, local_step(): pl.pallas_call(functools.partial(step_kernel, n), out_shape=(pltpu.VMEM((...  59.2 us
    pallas_call x1, Pallas kernels, local_step(): pl.pallas_call(last_kernel, out_shape=(jax.ShapeDtypeStruct((batch, shard...  5.05 us

profile of v3, /device:TPU:113, one launch (start us, length us, event | category | flops | bytes accessed | tf_op | source)
XLA Modules:
  0.0 64.9 jit_solution(11708903937179072080)
XLA Ops:
  0.6 59.2 %decode_step.1 = (bf16[48,512]{1,0:T(8,128)(2,1)S(1)}, bf16[6528,512]{1,0:T(8,128)(2,1)S(1)}, bf16[2,48,64,448]{3,2,1,0:T(8,128)(2,1)S(1)}, bf16[2,48,64,448]{3,2,1,0:T(8,128)(2,1)S(1)}) custom-call(s32[1,48]{1,0:T(1,128)} %bitcast.40, s32[1,48]{1,0:T(1,128)} %bitcast.41, f32[2,3,1,64]{3,2,1,0:T(1,128)} %in_bias.1, f32[3,2,512]{2,1,0:T(2,128)} %bitcast.39, ...), custom_call_target="tpu_custom_call" | custom-call | tf_op jit(solution)/shard_map/decode_step/pallas_call | solution.py:385
  59.8 5.0 %last.1 = (f32[48,6528]{1,0:T(8,128)}, bf16[2,48,64,448]{3,2,1,0:T(8,128)(2,1)}, bf16[2,48,64,448]{3,2,1,0:T(8,128)(2,1)}) custom-call(bf16[48,512]{1,0:T(8,128)(2,1)S(1)} %get-tuple-element.10.final, bf16[6528,512]{1,0:T(8,128)(2,1)S(1)} %get-tuple-element.11.table, bf16[2,48,64,448]{3,2,1,0:T(8,128)(2,1)S(1)} %get-tuple-element.12.sk, ...), custom_call_target="tpu_custom_call" | custom-call | tf_op jit(solution)/shard_map/last/pallas_call | solution.py:429

commit v4 on v3

--- a/solution.py
+++ b/solution.py
@@ -9,7 +9,9 @@
 
 MESH = pl.DeviceIdType.MESH
 LANES = 128
+GROUP = 8
 CHUNKS = 8
+SMALL = 7
 STEP_VMEM = 42 * 1024 * 1024
 LAST_VMEM = 8 * 1024 * 1024
 F32 = jnp.float32
@@ -33,19 +35,26 @@
 
 
 def step_kernel(
-    n, tokens, positions, in_bias, out_bias, b_fc1, ln_layers, ln_final,
+    n, *refs,
+):
+    small_hbm, refs = refs[:SMALL], refs[SMALL:]
+    (
     embed, pos_table, w_qkv_hbm, w_cq_hbm, fc1_hbm, fc2_hbm, w_out, self_k, self_v, cross_k, cross_v,
     final_out, table, sk, sv,
     ck, cv, wo_full, pos_vmem, w_qkv, w_cq, fc1, fc2, emb_own, emb_partner, emb_chip, emb_slots, o_slots,
     rs_src, rs_slots, ag_slots, one_hot, columns, x, places, fresh,
     sem_e, sem_p, sem_own, sem_self, sem_cross, sem_w, pair_send, pair_recv, emb_send, emb_recv,
     o_send, o_recv, rs_send, rs_recv, ag_send, ag_recv, w_send, w_recv,
-):
+    small, sem_small,
+    ) = (*refs[:-SMALL - 1], refs[-SMALL - 1 : -1], refs[-1])
+    tokens, positions, in_bias, out_bias, b_fc1, ln_layers, ln_final = small
+    small_loads = [pltpu.make_async_copy(a, b, sem_small.at[i]) for i, (a, b) in enumerate(zip(small_hbm, small))]
+    for c in small_loads:
+        c.start()
     layers, batch = sk.shape[0], sk.shape[1]
     head, ctx = sk.shape[2], sk.shape[3]
     width = table.shape[1]
     half, block = batch // 2, width // (n // 2)
-    span = half * head
     me = lax.axis_index("tp")
     core, chip = lax.rem(me, 2), lax.div(me, 2)
     partner = me + 1 - 2 * core
@@ -123,6 +132,8 @@
         j = lax.broadcasted_iota(jnp.int32, (batch, batch), 1)
         return jnp.sum(jnp.where(i == j, jnp.broadcast_to(row.astype(F32), (batch, batch)), 0.0), axis=1, keepdims=True)
 
+    for c in small_loads:
+        c.wait()
     token = as_column(tokens[...]).astype(jnp.int32) - me * table.shape[0]
     place = as_column(positions[...]).astype(jnp.int32)
     pl.semaphore_wait(barrier, n - 1)
@@ -149,42 +160,60 @@
     pair_sum = picked + emb_partner[...].astype(F32)
     for r in range(2):
         emb_chip[r] = pair_sum[r * half : (r + 1) * half].astype(BF16)
-    others = [k for k in order]
-    sends = []
-    for dc in (n // 4, *[d for d in range(1, n // 2) if d != n // 4]):
-        for other in range(2):
-            to = lax.rem(chip + dc, n // 2) * 2 + lax.rem(core + other, 2)
-            sends.append(remote(emb_chip.at[core], emb_slots.at[chip, core], emb_send.at[dc, other], emb_recv.at[chip, core], to))
-    for c in sends:
-        c.start()
+    cols = width // 2
+    distances = (n // 4, *[d for d in range(1, n // 2) if d != n // 4])
+
+    def table_hop(dc, other, r):
+        to = lax.rem(chip + dc, n // 2) * 2 + lax.rem(core + other, 2)
+        here = pl.ds(pl.multiple_of(core * cols, LANES), cols)
+        return remote(emb_chip.at[r, :, here], emb_slots.at[chip, r, :, here], emb_send.at[r, dc, other], emb_recv.at[r, chip, core], to)
+
+    for r in range(2):
+        for dc in distances:
+            for other in range(2):
+                table_hop(dc, other, r).start()
     weights_start(1)
-    x_parts = [pair_sum[r * half : (r + 1) * half] for r in range(2)]
-    for dc in range(1, n // 2):
-        far = lax.rem(chip + dc, n // 2)
+    for r in range(2):
+        x[r] = pair_sum[r * half : (r + 1) * half] + pos_rows[r * half : (r + 1) * half]
+        places[r] = jnp.broadcast_to(place[r * half : (r + 1) * half], (half, LANES))
+
+    def table_stage(r):
+        total = x[r]
+        for dc in reversed(distances):
+            far = lax.rem(chip + dc, n // 2)
+            for c in range(2):
+                slot = emb_slots.at[far, r, :, c * cols : (c + 1) * cols]
+                remote(slot, slot, emb_send.at[r, dc, c], emb_recv.at[r, far, c], far * 2 + c).wait_recv()
+            total = total + emb_slots[far, r].astype(F32)
+        x[r] = total
+
+    def table_sent():
         for r in range(2):
-            remote(emb_chip.at[0], emb_slots.at[far, r], emb_send.at[dc, r], emb_recv.at[far, r], far * 2 + r).wait_recv()
-            x_parts[r] = x_parts[r] + emb_slots[far, r].astype(F32)
-    for c in sends:
-        c.wait_send()
-    for r in range(2):
-        x[r] = x_parts[r] + pos_rows[r * half : (r + 1) * half]
-        places[r] = jnp.broadcast_to(place[r * half : (r + 1) * half], (half, LANES))
-
-    diagonal = lax.broadcasted_iota(jnp.int32, (half, span), 0) == lax.div(lax.broadcasted_iota(jnp.int32, (half, span), 1), head)
+            for dc in distances:
+                for other in range(2):
+                    table_hop(dc, other, r).wait_send()
+
+    span = GROUP * head
+    diagonal = lax.broadcasted_iota(jnp.int32, (GROUP, span), 0) == lax.div(lax.broadcasted_iota(jnp.int32, (GROUP, span), 1), head)
 
     def attend(q, keys, vals, finish):
         length = keys.shape[2]
-        wide = jnp.where(diagonal, jnp.concatenate([q] * half, axis=1), 0).astype(BF16)
-        scores = dot_nn(wide, keys[...].reshape(span, length))
-        weights, extra = finish(scores * (head ** -0.5))
-        full = jnp.where(diagonal, dot_nt(weights, vals[...].reshape(span, length)), 0.0)
-        total = full[:, :LANES]
-        for c in range(LANES, span, LANES):
-            total = total + full[:, c : c + LANES]
-        out = total[:, :head]
-        for c in range(head, LANES, head):
-            out = out + total[:, c : c + head]
-        return out + extra
+        q = q.astype(F32)
+        groups = [slice(g, g + GROUP) for g in range(0, half, GROUP)]
+        wide = [jnp.where(diagonal, jnp.concatenate([q[rows]] * GROUP, axis=1), 0.0).astype(BF16) for rows in groups]
+        scores = [dot_nn(w, keys[rows].reshape(span, length)) for w, rows in zip(wide, groups)]
+        finished = [finish(s * (head ** -0.5), rows) for s, rows in zip(scores, groups)]
+        out = []
+        for (weights, extra), rows in zip(finished, groups):
+            full = jnp.where(diagonal, dot_nt(weights, vals[rows].reshape(span, length)), 0.0)
+            total = full[:, :LANES]
+            for c in range(LANES, span, LANES):
+                total = total + full[:, c : c + LANES]
+            mixed = total[:, :head]
+            for c in range(head, LANES, head):
+                mixed = mixed + total[:, c : c + head]
+            out.append(mixed + extra)
+        return jnp.concatenate(out, axis=0)
 
     def head_slots(e, r):
         return o_slots.at[e, r], o_send.at[e, r], o_recv.at[e, r]
@@ -194,13 +223,16 @@
         slots[me] = attended.astype(BF16)
         send_all(lambda j: slots.at[me], slots, send, recv)
 
-    def gathered_heads(e, r):
-        slots, send, recv = head_slots(e, r)
-        wait_all(slots, send, recv)
-        return jnp.concatenate([slots[j].astype(F32) for j in range(n)], axis=1).astype(BF16)
-
-    def project(l, a, heads):
-        return dot_nn(heads, wo_full[l, a].reshape(n * head, width)).astype(BF16).astype(F32)
+    def project(l, a, r):
+        slots, send, recv = head_slots(2 * l + a, r)
+        total = dot_nn(slots[me], wo_full[l, a, me])
+        for k in reversed(order):
+            j = peer(k)
+            remote(slots.at[j], slots.at[j], send.at[k], recv.at[j], j).wait_recv()
+            total = total + dot_nn(slots[j], wo_full[l, a, j])
+        for k in order:
+            remote(slots.at[me], slots.at[me], send.at[k], recv.at[me], peer(k)).wait_send()
+        return total.astype(BF16).astype(F32)
 
     def put_columns(l):
         eye = (lax.broadcasted_iota(jnp.int32, (head, head), 0) == lax.broadcasted_iota(jnp.int32, (head, head), 1))
@@ -233,15 +265,16 @@
         fresh[0, r] = k_new.astype(F32)
         fresh[1, r] = v_new.astype(F32)
         here = places[r][:, :1]
-        new_score = jnp.sum(q.astype(F32) * k_new.astype(F32), axis=-1, keepdims=True) * (head ** -0.5)
-
-        def finish(s):
-            s = jnp.where(lax.broadcasted_iota(jnp.int32, s.shape, 1) < here, s, -1e30)
+        all_new = jnp.sum(q.astype(F32) * k_new.astype(F32), axis=-1, keepdims=True) * (head ** -0.5)
+
+        def finish(s, rows):
+            new_score = all_new[rows]
+            s = jnp.where(lax.broadcasted_iota(jnp.int32, s.shape, 1) < here[rows], s, -1e30)
             peak = jnp.maximum(jnp.max(s, axis=-1, keepdims=True), new_score)
             e = jnp.exp(s - peak)
             e_new = jnp.exp(new_score - peak)
             total = jnp.sum(e, axis=-1, keepdims=True) + e_new
-            return (e / total).astype(BF16), (e_new / total).astype(BF16).astype(F32) * v_new.astype(F32)
+            return (e / total).astype(BF16), (e_new / total).astype(BF16).astype(F32) * v_new.astype(F32)[rows]
 
         attended = attend(q, sk.at[l, rows], sv.at[l, rows], finish)
         exchange_heads(2 * l, r, attended)
@@ -249,11 +282,11 @@
     def cross_stage(l, r):
         ln = ln_layers[l]
         rows = pl.ds(r * half, half)
-        x[r] = x[r] + project(l, 0, gathered_heads(2 * l, r)) + out_bias[0, l : l + 1]
+        x[r] = x[r] + project(l, 0, r) + out_bias[0, l : l + 1]
         h = layer_norm(x[r], ln[1, 0:1], ln[1, 1:2])
         q = (dot_nt(h, w_cq[l]) + in_bias[l, 2]).astype(BF16)
 
-        def finish(s):
+        def finish(s, rows):
             e = jnp.exp(s - jnp.max(s, axis=-1, keepdims=True))
             return (e / jnp.sum(e, axis=-1, keepdims=True)).astype(BF16), 0.0
 
@@ -262,7 +295,7 @@
 
     def mlp_stage(l, r):
         ln = ln_layers[l]
-        x[r] = x[r] + project(l, 1, gathered_heads(2 * l + 1, r)) + out_bias[1, l : l + 1]
+        x[r] = x[r] + project(l, 1, r) + out_bias[1, l : l + 1]
         h = layer_norm(x[r], ln[2, 0:1], ln[2, 1:2])
         hidden = dot_nn(h, fc1[l]) + b_fc1[l : l + 1]
         active = (0.5 * hidden * (1.0 + lax.erf(hidden * (0.5 ** 0.5)))).astype(BF16)
@@ -303,6 +336,10 @@
         for k in order:
             remote(ag_slots.at[l, me], ag_slots.at[l, me], ag_send.at[l, k], ag_recv.at[l, me], peer(k)).wait_send()
 
+    def first_stage(l, r):
+        table_stage(r)
+        self_stage(l, r)
+
     def next_stage(l, r):
         add_stage(l - 1, r)
         self_stage(l, r)
@@ -314,7 +351,8 @@
     own[0].wait()
     for c in self_loads[0]:
         c.wait()
-    both(self_stage, 0)
+    both(first_stage, 0)
+    table_sent()
     for l in range(layers):
         last = l + 1 == layers
         weights_forward(2 * l)
@@ -382,10 +420,11 @@
         hbm = pl.BlockSpec(memory_space=pl.ANY)
         sem = pltpu.SemaphoreType.DMA
         cache_rows = (layers, batch, head, ctx)
+        small = (tokens[None], positions[None], in_bias, jnp.transpose(out_bias, (1, 0, 2)), b_fc1, ln_layers, ln_final)
         final_hidden, table, sk, sv = pl.pallas_call(
             functools.partial(step_kernel, n),
             out_shape=(pltpu.VMEM((batch, width), BF16), pltpu.VMEM((shard_rows, width), BF16), pltpu.VMEM(cache_rows, BF16), pltpu.VMEM(cache_rows, BF16)),
-            in_specs=[vmem] * 7 + [hbm] * 11,
+            in_specs=[hbm] * (SMALL + 11),
             out_specs=(vmem, vmem, vmem, vmem),
             scratch_shapes=[
                 pltpu.VMEM((layers, batch, head, frames), BF16),
@@ -410,14 +449,16 @@
                 pltpu.VMEM((2, half, LANES), jnp.int32),
                 pltpu.VMEM((2, 2, half, head), F32),
                 sem((CHUNKS,)), sem, sem((4,)), sem((layers, 2)), sem((layers, 2)), sem((2 * layers,)),
-                sem, sem, sem((n // 2, 2)), sem((n // 2, 2)),
+                sem, sem, sem((2, n // 2, 2)), sem((2, n // 2, 2)),
                 sem((2 * layers, 2, n)), sem((2 * layers, 2, n)), sem((layers, n)), sem((layers, n)), sem((layers, n)), sem((layers, n)),
                 sem((2 * layers, n)), sem((2 * layers, n)),
+                *[pltpu.VMEM(a.shape, a.dtype) for a in small],
+                sem((SMALL,)),
             ],
             compiler_params=pltpu.CompilerParams(collective_id=0, has_side_effects=True, vmem_limit_bytes=STEP_VMEM),
             name="decode_step",
         )(
-            tokens[None], positions[None], in_bias, jnp.transpose(out_bias, (1, 0, 2)), b_fc1, ln_layers, ln_final,
+            *small,
             embed_table, pos_table, jnp.transpose(w_qkv[:, :, :, 0, :], (0, 2, 3, 1)), jnp.transpose(w_cq[:, :, 0, :], (0, 2, 1)),
             w_fc1, w_fc2, w_out[:, :, 0],
             by_place(self_keys), by_place(self_vals), by_place(cross_keys), by_place(cross_vals),

time: 65 us -> 60.8 us (0.935)
  Pallas kernels: 64.2 us -> 60.1 us
    pallas_call x1, Pallas kernels: 59.2 us -> 55.1 us  [local_step(): pl.pallas_call(functools.partial(step_kernel, n), out_shape=(pltpu.VMEM((...]
where the time goes in v4:
time: 60.8 us
  Pallas kernels  60.1 us (99%)
  between operations  0.65 us (1%)
    pallas_call x1, Pallas kernels, local_step(): pl.pallas_call(functools.partial(step_kernel, n), out_shape=(pltpu.VMEM((...  55.1 us
    pallas_call x1, Pallas kernels, local_step(): pl.pallas_call(last_kernel, out_shape=(jax.ShapeDtypeStruct((batch, shard...  5.05 us

profile of v4, /device:TPU:113, one launch (start us, length us, event | category | flops | bytes accessed | tf_op | source)
XLA Modules:
  0.0 60.8 jit_solution(8442978478097751141)
XLA Ops:
  0.6 55.1 %decode_step.1 = (bf16[48,512]{1,0:T(8,128)(2,1)S(1)}, bf16[6528,512]{1,0:T(8,128)(2,1)S(1)}, bf16[2,48,64,448]{3,2,1,0:T(8,128)(2,1)S(1)}, bf16[2,48,64,448]{3,2,1,0:T(8,128)(2,1)S(1)}) custom-call(s32[1,48]{1,0:T(1,128)} %bitcast.40, s32[1,48]{1,0:T(1,128)} %bitcast.41, f32[2,3,1,64]{3,2,1,0:T(1,128)} %refs_2_.1, f32[3,2,512]{2,1,0:T(2,128)} %bitcast.39, ...), custom_call_target="tpu_custom_call" | custom-call | tf_op jit(solution)/shard_map/decode_step/pallas_call | solution.py:424
  55.7 5.0 %last.1 = (f32[48,6528]{1,0:T(8,128)}, bf16[2,48,64,448]{3,2,1,0:T(8,128)(2,1)}, bf16[2,48,64,448]{3,2,1,0:T(8,128)(2,1)}) custom-call(bf16[48,512]{1,0:T(8,128)(2,1)S(1)} %get-tuple-element.10.final, bf16[6528,512]{1,0:T(8,128)(2,1)S(1)} %get-tuple-element.11.table, bf16[2,48,64,448]{3,2,1,0:T(8,128)(2,1)S(1)} %get-tuple-element.12.sk, ...), custom_call_target="tpu_custom_call" | custom-call | tf_op jit(solution)/shard_map/last/pallas_call | solution.py:470

commit v5 on v4

--- a/solution.py
+++ b/solution.py
@@ -9,7 +9,7 @@
 
 MESH = pl.DeviceIdType.MESH
 LANES = 128
-GROUP = 8
+GROUP = 4
 CHUNKS = 8
 SMALL = 7
 STEP_VMEM = 42 * 1024 * 1024

time: 60.8 us -> 60.8 us (level)
  no operation moved by 1% of the time
where the time goes in v5:
time: 60.8 us; the launch traced here: 60.7 us
  Pallas kernels  60 us (99%)
  between operations  0.65 us (1%)
    pallas_call x1, Pallas kernels, local_step(): pl.pallas_call(functools.partial(step_kernel, n), out_shape=(pltpu.VMEM((...  55 us
    pallas_call x1, Pallas kernels, local_step(): pl.pallas_call(last_kernel, out_shape=(jax.ShapeDtypeStruct((batch, shard...  5.05 us

profile of v5, /device:TPU:113, one launch (start us, length us, event | category | flops | bytes accessed | tf_op | source)
XLA Modules:
  0.0 60.7 jit_solution(11831240019836540466)
XLA Ops:
  0.6 55.0 %decode_step.1 = (bf16[48,512]{1,0:T(8,128)(2,1)S(1)}, bf16[6528,512]{1,0:T(8,128)(2,1)S(1)}, bf16[2,48,64,448]{3,2,1,0:T(8,128)(2,1)S(1)}, bf16[2,48,64,448]{3,2,1,0:T(8,128)(2,1)S(1)}) custom-call(s32[1,48]{1,0:T(1,128)} %bitcast.40, s32[1,48]{1,0:T(1,128)} %bitcast.41, f32[2,3,1,64]{3,2,1,0:T(1,128)} %refs_2_.1, f32[3,2,512]{2,1,0:T(2,128)} %bitcast.39, ...), custom_call_target="tpu_custom_call" | custom-call | tf_op jit(solution)/shard_map/decode_step/pallas_call | solution.py:424
  55.6 5.0 %last.1 = (f32[48,6528]{1,0:T(8,128)}, bf16[2,48,64,448]{3,2,1,0:T(8,128)(2,1)}, bf16[2,48,64,448]{3,2,1,0:T(8,128)(2,1)}) custom-call(bf16[48,512]{1,0:T(8,128)(2,1)S(1)} %get-tuple-element.10.final, bf16[6528,512]{1,0:T(8,128)(2,1)S(1)} %get-tuple-element.11.table, bf16[2,48,64,448]{3,2,1,0:T(8,128)(2,1)S(1)} %get-tuple-element.12.sk, ...), custom_call_target="tpu_custom_call" | custom-call | tf_op jit(solution)/shard_map/last/pallas_call | solution.py:470
